TPU v7x, 8 devices: a whole 2x2x1 slice. The times are simulated.
8 devices in a mesh: pp: 2 (over z, y), tp: 4 (over x, core).
Axes of the slice: x: 2, y: 2, z: 1, core: 2. Of those that a mesh axis runs over, the one named last changes fastest.
Arguments:
- activations: bfloat16 [256, 28, 28, 256], P(('pp', 'tp'))
- conv_w: bfloat16 [3, 3, 256, 256], P(None, None, 'tp')
- bn_scale: float32 [256], P('tp')
- bn_shift: float32 [256], P('tp')
Outputs:
- output: bfloat16 [256, 28, 28, 256], P('pp', None, None, 'tp')
All inputs are finite; a program needn't handle non-finite values.
Results may differ from a plain program's by a relative error of at most 0.001.
Values are sent between devices in bfloat16 or wider.
A program may use at most 1 GiB of HBM per device.

v0:
```python
import jax
import jax.numpy as jnp
from jax import lax
from jax.sharding import PartitionSpec as P

CONV_DIMS = ("NHWC", "HWIO", "NHWC")


def solution(mesh):
    half_pp = mesh.shape["pp"] // 2
    send_pairs = [(source, source + half_pp) for source in range(half_pp)]

    def local_step(act_block, w_shard, scale_shard, shift_shard):
        by_channel = lax.all_to_all(act_block, "tp", 3, 0, tiled=True)
        moved_in = lax.ppermute(by_channel, "pp", perm=send_pairs)
        partial_sum = lax.conv_general_dilated(moved_in, w_shard, (1, 1), "SAME", dimension_numbers=CONV_DIMS, preferred_element_type=jnp.float32)
        pre_act = lax.psum_scatter(partial_sum, "tp", scatter_dimension=3, tiled=True)
        y_val = pre_act * scale_shard + shift_shard
        stage_mask = (lax.axis_index("pp") >= half_pp).astype(jnp.float32)
        return (jnp.maximum(y_val, 0.0) * stage_mask).astype(jnp.bfloat16)

    return jax.shard_map(local_step, mesh=mesh, in_specs=(P(("pp", "tp")), P(None, None, "tp", None), P("tp"), P("tp")), out_specs=P("pp", None, None, "tp"), check_vma=False)
```

profile of v0, /device:TPU:1, one launch (start us, length us, event | category | flops | bytes accessed | tf_op | source)
XLA Modules:
  0.0 1480.1 jit_solution(14406006578042053230)
XLA Ops:
  6.5 0.0 copy-start
  6.5 0.0 reduce-scatter.2.cloned.1.call-start
  6.5 77.3 %copy.8 = bf16[32,28,28,256]{0,2,1,3:T(8,128)(2,1)} copy(bf16[32,28,28,256]{3,0,2,1:T(8,128)(2,1)} %param.4) | data formatting | bytes 25690112 | tf_op args[0]
  83.8 71.0 %reshape.2 = bf16[4,2,802816]{2,1,0:T(2,128)(2,1)} reshape(bf16[256,28,28,32]{3,2,1,0:T(8,128)(2,1)} %bitcast.9) | data formatting | bytes 25690112
  154.9 150.0 %all_to_all.18 = bf16[4,2,802816]{2,1,0:T(2,128)(2,1)} all-to-all(bf16[4,2,802816]{2,1,0:T(2,128)(2,1)} %reshape.2), channel_id=1, replica_groups=mesh['pp'=2,'tp'=4] {'tp'}, dimensions={0} | all-to-all | bytes 25690112 | tf_op jit(solution)/shard_map/all_to_all | solution.py:14
  304.8 68.9 %reshape.3 = bf16[256,28,28,32]{3,2,1,0:T(8,128)(2,1)} reshape(bf16[4,2,802816]{2,1,0:T(2,128)(2,1)} %all_to_all.18) | data formatting | bytes 25690112
  373.7 73.8 %copy.9 = bf16[32,28,28,4,64]{4,0,3,2,1:T(8,128)(2,1)} copy(bf16[32,28,28,4,64]{0,2,1,4,3:T(8,128)(2,1)} %bitcast.8) | data formatting | bytes 25690112 | tf_op jit(solution)/shard_map/all_to_all | solution.py:14
  447.5 25.2 %copy.10 = bf16[128,28,28,64]{0,3,2,1:T(8,128)(2,1)} copy(bf16[128,28,28,64]{3,0,2,1:T(8,128)(2,1)} %bitcast.10) | data formatting | bytes 25690112 | tf_op jit(solution)/shard_map/all_to_all | solution.py:14
  472.6 8.4 collective-permute-start
  481.0 269.6 %collective-permute-done = bf16[128,28,28,64]{0,3,2,1:T(8,128)(2,1)} collective-permute-done((bf16[128,28,28,64]{0,3,2,1:T(8,128)(2,1)}, bf16[128,28,28,64]{0,3,2,1:T(8,128)(2,1)}, u32[]{:S(2)}, u32[]{:S(2)}) %collective-permute-start) | collective-permute-done | bytes 12845088 | tf_op jit(solution)/shard_map/ppermute | solution.py:15
  750.6 0.0 copy-done
  750.6 51.5 %fusion = f32[128,28,28,256]{0,3,2,1:T(8,128)} fusion(bf16[128,28,28,64]{0,3,2,1:T(8,128)(2,1)} %collective-permute-done, bf16[3,3,64,256]{3,2,1,0:T(8,128)(2,1)S(1)} %copy-done), kind=kOutput, calls=%fused_computation.1 | convolution fusion | flops 28202500096 | bytes 115900416 | tf_op jit(solution)/shard_map/conv_general_dilated | solution.py:16
  802.1 0.0 copy-start.2
  802.1 0.0 copy-start.3
  802.1 0.0 reduce-scatter.2.cloned.1.call-update
  802.1 0.0 copy-start.1
  802.1 654.5 %reduce-scatter.2.cloned.1.call-done = f32[128,28,28,64]{0,3,2,1:T(8,128)} async-done(((f32[128,28,28,256]{0,3,2,1:T(8,128)}), f32[128,28,28,64]{0,3,2,1:T(8,128)}) %reduce-scatter.2.cloned.1.call-update) | async-done | bytes 25690128 | tf_op jit(solution)/shard_map/reduce_scatter | solution.py:17
  1456.6 0.0 copy-done.2
  1456.6 0.0 copy-done.3
  1456.6 16.7 %multiply_convert_fusion = bf16[128,28,28,64]{0,3,2,1:T(8,128)(2,1)} fusion(f32[128,28,28,64]{0,3,2,1:T(8,128)} %reduce-scatter.2.cloned.1.call-done, f32[]{:T(128)S(6)} %convert_element_type.6, f32[64]{0:T(128)S(1)} %copy-done.2, f32[64]{0:T(128)S(1)} %copy-done.3), kind=kLoop, calls=%fused_computation | loop fusion | flops 32112640 | bytes 38535684 | tf_op jit(solution)/shard_map/convert_element_type | solution.py:20
  1473.2 0.0 copy-done.1
Async XLA Ops:
  6.5 744.1 %copy-start = (bf16[3,3,64,256]{3,2,1,0:T(8,128)(2,1)S(1)}, bf16[3,3,64,256]{3,2,1,0:T(8,128)(2,1)}, u32[]{:S(2)}) copy-start(bf16[3,3,64,256]{3,2,1,0:T(8,128)(2,1)} %param.5) | copy-start | bytes 884740
  6.5 1450.0 %reduce-scatter.2.cloned.1.call-start = ((), (), s32[]{:S(2)}) async-start(), calls=%async_computation.2 | async-start | bytes 128450560 | tf_op jit(solution)/shard_map/reduce_scatter | solution.py:17
  472.6 278.0 %collective-permute-start = (bf16[128,28,28,64]{0,3,2,1:T(8,128)(2,1)}, bf16[128,28,28,64]{0,3,2,1:T(8,128)(2,1)}, u32[]{:S(2)}, u32[]{:S(2)}) collective-permute-start(bf16[128,28,28,64]{0,3,2,1:T(8,128)(2,1)} %copy.10), channel_id=1, source_target_pairs={{0,4},{1,5},{2,6},{3,7}} | collective-permute-start | bytes 38535176 | tf_op jit(solution)/shard_map/ppermute | solution.py:15
  802.1 654.5 %copy-start.2 = (f32[64]{0:T(128)S(1)}, f32[64]{0:T(128)}, u32[]{:S(2)}) copy-start(f32[64]{0:T(128)} %param.7) | copy-start | bytes 772
  802.1 654.5 %copy-start.3 = (f32[64]{0:T(128)S(1)}, f32[64]{0:T(128)}, u32[]{:S(2)}) copy-start(f32[64]{0:T(128)} %param.6) | copy-start | bytes 772
  802.1 671.1 %copy-start.1 = (bf16[3,3,64,256]{3,2,1,0:T(8,128)(2,1)S(1)}, bf16[3,3,64,256]{3,2,1,0:T(8,128)(2,1)}, u32[]{:S(2)}) copy-start(bf16[3,3,64,256]{3,2,1,0:T(8,128)(2,1)} %param.5) | copy-start | bytes 884740
Sparse Core Ops, SparseCore 0:
  802.2 654.3 reduce-scatter.1
where the time goes:
time: 1480 us
  waiting for transfers between devices  924 us (62%)
  local copies, waits for them, and re-layouts  316 us (21%)
  blocking collectives  150 us (10%)
  matrix products  51.5 us (3%)
  other arithmetic  16.7 us (1%)
    reduce_scatter x1, waiting for transfers between devices, local_step(): lax.psum_scatter(partial_sum, 'tp', scatter_dimension=3, tiled=True)  654 us
    ppermute x1, waiting for transfers between devices, local_step(): moved_in = lax.ppermute(by_channel, 'pp', perm=send_pairs)  270 us
    unnamed x11, local copies, waits for them, and re-layouts  217 us
    all_to_all x1, blocking collectives, local_step(): by_channel = lax.all_to_all(act_block, 'tp', 3, 0, tiled=True)  150 us
    all_to_all x2, local copies, waits for them, and re-layouts, local_step(): by_channel = lax.all_to_all(act_block, 'tp', 3, 0, tiled=True)  98.9 us
    conv_general_dilated x1, matrix products, local_step(): lax.conv_general_dilated(moved_in, w_shard, (1, 1), 'SAME', dimension_num...  51.5 us
  transfers between devices with their start and end apart: 2, of which 2 were waited for; matrix products, arithmetic and copies ran while one was open for 0% of the time, Pallas kernels for 0%

commit v1 on v0

v1 whole, which is shorter than its diff:
```python
import functools

import jax
import jax.numpy as jnp
from jax import lax
from jax.experimental import pallas as pl
from jax.experimental.pallas import tpu as pltpu
from jax.sharding import PartitionSpec as P

MESH = pl.DeviceIdType.MESH
H, W, C = 28, 28, 256
N_LOC = 32
TP = 4
CB = C // TP
LANES = 128
PAIRS = W // 2
Q = 7
FLUSH = 14
VL = 46 * 2**20


def kernel(act, w, scale, shift, out, xpad, buf, wf, sb, xsem, wlsem, wssem, wrsem, bssem, brsem, ssem, rsem):
    pp, tp = lax.axis_index("pp"), lax.axis_index("tp")
    chip, core = tp // 2, tp % 2
    far = 1 - chip

    def w_copy(owner, part, half, slot, target):
        return pltpu.make_async_remote_copy(
            src_ref=w.at[:, :, pl.ds(pl.multiple_of(half * LANES, LANES), LANES)],
            dst_ref=wf.at[half, :, owner],
            send_sem=wssem.at[part, slot],
            recv_sem=wrsem.at[part, owner],
            device_id=target,
            device_id_type=MESH,
        )

    def w_local(half, part):
        return pltpu.make_async_copy(
            w.at[:, :, pl.ds(pl.multiple_of(half * LANES, LANES), LANES)], wf.at[half, :, tp], wlsem.at[part])

    def x_copy(h):
        return pltpu.make_async_copy(act.at[h], xpad.at[h + 1, pl.ds(1, W)], xsem.at[h])

    def b_copy(k, owner):
        return pltpu.make_async_remote_copy(
            src_ref=sb.at[tp], dst_ref=sb.at[tp], send_sem=bssem.at[k], recv_sem=brsem.at[owner],
            device_id=(0, lax.rem(tp + k, TP)), device_id_type=MESH)

    def z_copy(h, t, owner):
        return pltpu.make_async_remote_copy(
            src_ref=buf.at[h, :, t], dst_ref=buf.at[h, :, owner], send_sem=ssem.at[h, t], recv_sem=rsem.at[h, owner],
            device_id=(1, t), device_id_type=MESH)

    @pl.when(pp == 0)
    def _():
        for part in range(2):
            w_local(chip if part == 0 else far, part).start()

        def start_x(h, _):
            x_copy(h).start()
            return 0
        lax.fori_loop(0, H, start_x, 0)
        sb[tp, 0:1, :] = jnp.concatenate([scale[...], scale[...]], axis=1)
        sb[tp, 1:2, :] = jnp.concatenate([shift[...], shift[...]], axis=1)

    barrier = pltpu.get_barrier_semaphore()
    for d in range(1, 2 * TP):
        other = lax.rem(pp * TP + tp + d, 2 * TP)
        pl.semaphore_signal(barrier, inc=1, device_id=(other // TP, other % TP), device_id_type=MESH)
    pl.semaphore_wait(barrier, 2 * TP - 1)

    def far_sends(act_on):
        for part in range(2):
            half = far if part == 0 else chip
            for c in range(2):
                act_on(w_copy(tp, part, half, c, (0, far * 2 + c)))

    def near_sends(act_on):
        for part in range(2):
            half = chip if part == 0 else far
            act_on(w_copy(tp, part, half, 2, (0, chip * 2 + 1 - core)))

    sends_far = jnp.logical_or(jnp.logical_and(pp == 0, core == 0), jnp.logical_and(pp == 1, core == 1))

    @pl.when(sends_far)
    def _():
        far_sends(lambda c: c.start())

    @pl.when(pp == 0)
    def _():
        near_sends(lambda c: c.start())
        for k in range(1, TP):
            b_copy(k, tp).start()

        zero = jnp.zeros((W + 2, N_LOC, C), jnp.bfloat16)
        xpad[0] = zero
        xpad[H + 1] = zero
        xpad[:, 0] = zero
        xpad[:, W + 1] = zero

        for k in range(1, TP):
            b_copy(k, lax.rem(tp + k, TP)).wait_recv()

        lane = lax.broadcasted_iota(jnp.int32, (1, LANES), 1)
        low = lane < CB

        def wait_w(part, half):
            w_local(half, part).wait()
            for k in range(1, TP):
                owner = lax.rem(tp + k, TP)
                w_copy(owner, part, half, 0, (0, owner)).wait_recv()

        def step(h, half):
            sc = jnp.where(low, sb[2 * half, 0:1, :], sb[2 * half + 1, 0:1, :])
            sh = jnp.where(low, sb[2 * half, 1:2, :], sb[2 * half + 1, 1:2, :])

            def conv(w0):
                acc = None
                for a in range(3):
                    for b in range(3):
                        lhs = xpad[h + a, pl.ds(w0 + b, Q)].reshape(Q * N_LOC, C)
                        rhs = wf[half, 3 * a + b].reshape(C, LANES)
                        part = jnp.dot(lhs, rhs, preferred_element_type=jnp.float32)
                        acc = part if acc is None else acc + part
                return jnp.maximum(acc * sc + sh, 0.0)

            for q in range(PAIRS // Q):
                even, odd = conv(q * Q), conv(PAIRS + q * Q)
                first = jnp.where(low, even, pltpu.roll(odd, CB, 1)).astype(jnp.bfloat16)
                second = jnp.where(low, pltpu.roll(even, CB, 1), odd).astype(jnp.bfloat16)
                buf[h, pl.ds(q * Q, Q), 2 * half] = first.reshape(Q, N_LOC, LANES)
                buf[h, pl.ds(q * Q, Q), 2 * half + 1] = second.reshape(Q, N_LOC, LANES)
            for k in range(2):
                z_copy(h, 2 * half + k, tp).start()

        def row(h, _):
            @pl.when(h == 0)
            def _():
                x_copy(0).wait()

            @pl.when(h < H - 1)
            def _():
                x_copy(h + 1).wait()

            def both(j, _):
                half = jnp.where(j == 0, chip, far)

                @pl.when(h == 0)
                def _():
                    wait_w(j, half)
                step(h, half)
                return 0
            lax.fori_loop(0, 2, both, 0)
            return 0
        lax.fori_loop(0, H, row, 0)

        def clear(h, _):
            out[h] = jnp.zeros((W, CB, LANES), jnp.bfloat16)
            return 0
        lax.fori_loop(0, H, clear, 0)

        near_sends(lambda c: c.wait_send())
        for k in range(1, TP):
            b_copy(k, tp).wait_send()

        def drain(h, _):
            for t in range(TP):
                z_copy(h, t, tp).wait_send()
            return 0
        lax.fori_loop(0, H, drain, 0)

    @pl.when(sends_far)
    def _():
        far_sends(lambda c: c.wait_send())

    @pl.when(pp == 1)
    def _():
        def row(h, _):
            for s in range(TP):
                z_copy(h, s, s).wait_recv()

            def pair(p, _):
                block = buf[h, p].reshape(LANES, LANES)
                turned = block.T
                out[h, p] = turned[:CB]
                out[h, p + PAIRS] = turned[CB:]
                return 0
            lax.fori_loop(0, PAIRS, pair, 0)
            return 0
        lax.fori_loop(0, H, row, 0)


def flush(src, dst, sem):
    rows = H // FLUSH
    copies = [pltpu.make_async_copy(src.at[pl.ds(i * rows, rows)], dst.at[pl.ds(i * rows, rows)], sem.at[i])
              for i in range(FLUSH)]
    for c in copies:
        c.start()
    for c in copies:
        c.wait()


def solution(mesh):
    def local_step(act, w, scale, shift):
        x = jnp.transpose(act, (1, 2, 0, 3))
        dma = pltpu.SemaphoreType.DMA
        out = pl.pallas_call(
            kernel,
            out_shape=pltpu.VMEM((H, W, CB, LANES), jnp.bfloat16),
            in_specs=[pl.BlockSpec(memory_space=pl.ANY), pl.BlockSpec(memory_space=pl.ANY),
                      pl.BlockSpec(memory_space=pltpu.VMEM), pl.BlockSpec(memory_space=pltpu.VMEM)],
            out_specs=pl.BlockSpec(memory_space=pltpu.VMEM),
            scratch_shapes=[
                pltpu.VMEM((H + 2, W + 2, N_LOC, C), jnp.bfloat16),
                pltpu.VMEM((H, PAIRS, TP, N_LOC, LANES), jnp.bfloat16),
                pltpu.VMEM((2, 9, TP, C // TP, LANES), jnp.bfloat16),
                pltpu.VMEM((TP, 8, LANES), jnp.float32),
                dma((H,)), dma((2,)), dma((2, 3)), dma((2, TP)), dma((TP,)), dma((TP,)), dma((H, TP)), dma((H, TP)),
            ],
            compiler_params=pltpu.CompilerParams(collective_id=0, has_side_effects=True, vmem_limit_bytes=VL),
        )(x, w.reshape(9, C // TP, C), scale.reshape(1, CB), shift.reshape(1, CB))
        out = pl.pallas_call(
            flush,
            out_shape=jax.ShapeDtypeStruct((H, W, CB, LANES), jnp.bfloat16),
            in_specs=[pl.BlockSpec(memory_space=pltpu.VMEM)],
            out_specs=pl.BlockSpec(memory_space=pl.ANY),
            scratch_shapes=[dma((FLUSH,))],
            compiler_params=pltpu.CompilerParams(vmem_limit_bytes=2**20),
        )(out)
        return jnp.transpose(out, (3, 0, 1, 2))

    return jax.shard_map(local_step, mesh=mesh, in_specs=(P(("pp", "tp")), P(None, None, "tp", None), P("tp"), P("tp")),
                         out_specs=P("pp", None, None, "tp"), check_vma=False)
```

time: 1480 us -> 298 us (0.20)
  waiting for transfers between devices: 924 us -> 0 us
  local copies, waits for them, and re-layouts: 316 us -> 0 us
  Pallas kernels: 0 us -> 296 us
  blocking collectives: 150 us -> 0 us
  matrix products: 51.5 us -> 0 us
  other arithmetic: 16.7 us -> 0 us
    reduce_scatter x1 -> x0, waiting for transfers between devices: 654 us -> none  [local_step(): lax.psum_scatter(partial_sum, 'tp', scatter_dimension=3, tiled=True)]
    pallas_call x0 -> x2, Pallas kernels: none -> 296 us  [the longest x1 291 us: local_step(): pl.pallas_call(kernel, out_shape=pltpu.VMEM((H, W, CB, LANES), jnp.bfloat...]
    ppermute x1 -> x0, waiting for transfers between devices: 270 us -> none  [local_step(): moved_in = lax.ppermute(by_channel, 'pp', perm=send_pairs)]
    unnamed x11 -> x0, local copies, waits for them, and re-layouts: 217 us -> none
    all_to_all x1 -> x0, blocking collectives: 150 us -> none  [local_step(): by_channel = lax.all_to_all(act_block, 'tp', 3, 0, tiled=True)]
    all_to_all x2 -> x0, local copies, waits for them, and re-layouts: 98.9 us -> none  [local_step(): by_channel = lax.all_to_all(act_block, 'tp', 3, 0, tiled=True)]
    conv_general_dilated x1 -> x0, matrix products: 51.5 us -> none  [local_step(): lax.conv_general_dilated(moved_in, w_shard, (1, 1), 'SAME', dimension_num...]
    convert_element_type x1 -> x0, other arithmetic: 16.7 us -> none  [local_step(): return (jnp.maximum(y_val, 0.0) * stage_mask).astype(jnp.bfloat16)]
  transfers between devices with their start and end apart: 2 -> 0, of which waited for: 2 -> 0; matrix products, arithmetic and copies ran while one was open for 0% -> 0% of each run, Pallas kernels for 0% -> 0%
where the time goes in v1:
time: 298 us; the launch traced here: 296 us
  Pallas kernels  296 us (99%)
    pallas_call x1, Pallas kernels, local_step(): pl.pallas_call(kernel, out_shape=pltpu.VMEM((H, W, CB, LANES), jnp.bfloat...  291 us

profile of v1, /device:TPU:1, one launch (start us, length us, event | category | flops | bytes accessed | tf_op | source)
XLA Modules:
  0.0 296.2 jit_solution(12430616830916366241)
XLA Ops:
  0.0 291.5 %shard_map.46.src = bf16[28,28,64,128]{3,2,1,0:T(8,128)(2,1)S(1)} custom-call(bf16[28,28,32,256]{3,2,1,0:T(8,128)(2,1)} %bitcast.5, bf16[9,64,256]{2,1,0:T(8,128)(2,1)} %bitcast.6, f32[1,64]{1,0:T(1,128)} %bitcast.7, f32[1,64]{1,0:T(1,128)} %bitcast.8), custom_call_target="tpu_custom_call" | custom-call | tf_op jit(solution)/shard_map/pallas_call | solution.py:207
  291.5 4.8 %shard_map.47 = bf16[28,28,64,128]{3,2,1,0:T(8,128)(2,1)} custom-call(bf16[28,28,64,128]{3,2,1,0:T(8,128)(2,1)S(1)} %shard_map.46.src), custom_call_target="tpu_custom_call" | custom-call | tf_op jit(solution)/shard_map/pallas_call | solution.py:222

commit v2 on v1

v2 whole, which is shorter than its diff:
```python
import jax
import jax.numpy as jnp
from jax import lax
from jax.experimental import pallas as pl
from jax.experimental.pallas import tpu as pltpu
from jax.sharding import PartitionSpec as P

MESH = pl.DeviceIdType.MESH
H, W, C = 28, 28, 256
N_LOC = 32
TP = 4
CB = C // TP
LANES = 128
PAIRS = W // 2
Q = 7
G = 4
GROUPS = H // G
LAST = H - 1
FLUSH = 14
PARTS = ((0, 3, 6), (0, 0, 3), (1, 0, 9))


def kernel(act, w, scale, shift, out, xpad, buf, wf, sb, xsem, wlsem, wssem, wrsem, bssem, brsem, ssem, rsem, esem, fsem):
    pp, tp = lax.axis_index("pp"), lax.axis_index("tp")
    chip, core = tp // 2, tp % 2
    far = 1 - chip

    def half_of(sel, receiver):
        return receiver if sel == 0 else 1 - receiver

    def w_local(half):
        return pltpu.make_async_copy(
            w.at[:, :, pl.ds(pl.multiple_of(half * LANES, LANES), LANES)], wf.at[half, :, tp], wlsem.at[half])

    def w_copy(part, owner, slot, target):
        sel, tap, taps = PARTS[part]
        block = wf.at[half_of(sel, target // 2), pl.ds(tap, taps), owner]
        return pltpu.make_async_remote_copy(
            src_ref=block, dst_ref=block, send_sem=wssem.at[part, slot], recv_sem=wrsem.at[part, owner],
            device_id=(0, target), device_id_type=MESH)

    def x_copy(h):
        return pltpu.make_async_copy(act.at[h], xpad.at[h + 1, pl.ds(1, W)], xsem.at[h])

    def b_copy(k, owner):
        return pltpu.make_async_remote_copy(
            src_ref=sb.at[tp], dst_ref=sb.at[tp], send_sem=bssem.at[k], recv_sem=brsem.at[owner],
            device_id=(0, lax.rem(tp + k, TP)), device_id_type=MESH)

    def z_copy(h, rows, t, owner):
        return pltpu.make_async_remote_copy(
            src_ref=buf.at[pl.ds(h, rows), :, t], dst_ref=buf.at[pl.ds(h, rows), :, owner],
            send_sem=ssem.at[h, t], recv_sem=rsem.at[h, owner], device_id=(1, t), device_id_type=MESH)

    def z_part(i, q, t, owner):
        h = 0 if i == 0 else LAST
        return pltpu.make_async_remote_copy(
            src_ref=buf.at[h, pl.ds(q * Q, Q), t], dst_ref=buf.at[h, pl.ds(q * Q, Q), owner],
            send_sem=esem.at[i, q, t], recv_sem=fsem.at[i, q, owner], device_id=(1, t), device_id_type=MESH)

    sends_far = pp == core

    @pl.when(jnp.logical_or(pp == 0, sends_far))
    def _():
        w_local(0).start()
        w_local(1).start()

    @pl.when(pp == 0)
    def _():
        def start_x(h, _):
            x_copy(h).start()
            return 0
        lax.fori_loop(0, H, start_x, 0)
        sb[tp, 0:1, :] = jnp.concatenate([scale[...], scale[...]], axis=1)
        sb[tp, 1:2, :] = jnp.concatenate([shift[...], shift[...]], axis=1)

    barrier = pltpu.get_barrier_semaphore()
    for d in range(1, 2 * TP):
        other = lax.rem(pp * TP + tp + d, 2 * TP)
        pl.semaphore_signal(barrier, inc=1, device_id=(other // TP, other % TP), device_id_type=MESH)

    @pl.when(jnp.logical_or(pp == 0, sends_far))
    def _():
        w_local(0).wait()
        w_local(1).wait()
    pl.semaphore_wait(barrier, 2 * TP - 1)

    @pl.when(pp == 0)
    def _():
        for k in range(1, TP):
            b_copy(k, tp).start()

    def w_sends(act_on):
        for part in range(len(PARTS)):
            @pl.when(sends_far)
            def _():
                for c in range(2):
                    act_on(w_copy(part, tp, c, far * 2 + c))

            @pl.when(pp == 0)
            def _():
                act_on(w_copy(part, tp, 2, chip * 2 + 1 - core))

    w_sends(lambda c: c.start())

    @pl.when(pp == 0)
    def _():
        zero = jnp.zeros((W + 2, N_LOC, C), jnp.bfloat16)
        xpad[0] = zero
        xpad[H + 1] = zero
        xpad[:, 0] = zero
        xpad[:, W + 1] = zero

        for k in range(1, TP):
            b_copy(k, lax.rem(tp + k, TP)).wait_recv()

        low = lax.broadcasted_iota(jnp.int32, (1, LANES), 1) < CB

        def wait_w(part):
            for k in range(1, TP):
                w_copy(part, lax.rem(tp + k, TP), 0, tp).wait_recv()

        def pixels(h, half, q, first_tap):
            sc = jnp.where(low, sb[2 * half, 0:1, :], sb[2 * half + 1, 0:1, :])
            sh = jnp.where(low, sb[2 * half, 1:2, :], sb[2 * half + 1, 1:2, :])

            def conv(w0):
                acc = None
                for tap in range(first_tap, 9):
                    lhs = xpad[h + tap // 3, pl.ds(w0 + tap % 3, Q)].reshape(Q * N_LOC, C)
                    part = jnp.dot(lhs, wf[half, tap].reshape(C, LANES), preferred_element_type=jnp.float32)
                    acc = part if acc is None else acc + part
                return jnp.maximum(acc * sc + sh, 0.0)

            even, odd = conv(q * Q), conv(PAIRS + q * Q)
            first = jnp.where(low, even, pltpu.roll(odd, CB, 1)).astype(jnp.bfloat16)
            second = jnp.where(low, pltpu.roll(even, CB, 1), odd).astype(jnp.bfloat16)
            buf[h, pl.ds(q * Q, Q), 2 * half] = first.reshape(Q, N_LOC, LANES)
            buf[h, pl.ds(q * Q, Q), 2 * half + 1] = second.reshape(Q, N_LOC, LANES)

        x_copy(0).wait()
        x_copy(1).wait()
        wait_w(0)
        for q in range(2):
            pixels(0, chip, q, 3)
            for k in range(2):
                z_part(0, q, 2 * chip + k, tp).start()
        wait_w(1)

        def step(i, _):
            g, r = i // (2 * G), i % (2 * G)
            own = r < G
            half = jnp.where(own, chip, far)
            h = g * G + r % G

            @pl.when(i == G)
            def _():
                wait_w(2)

            @pl.when(jnp.logical_and(own, h < LAST))
            def _():
                x_copy(h + 1).wait()

            for q in range(2):
                pixels(h, half, q, 0)

                @pl.when(h == LAST)
                def _():
                    for k in range(2):
                        z_part(1, q, 2 * half + k, tp).start()

            edge = jnp.logical_or(g == 0, g == GROUPS - 1)

            @pl.when(jnp.logical_and(edge, jnp.logical_and(h < LAST, h > 0)))
            def _():
                for k in range(2):
                    z_copy(h, 1, 2 * half + k, tp).start()

            @pl.when(h == 0)
            def _():
                for q in range(2):
                    for k in range(2):
                        z_part(0, q, 2 * half + k, tp).start()

            @pl.when(jnp.logical_and(jnp.logical_not(edge), r % G == G - 1))
            def _():
                for k in range(2):
                    z_copy(g * G, G, 2 * half + k, tp).start()
            return 0
        lax.fori_loop(1, 2 * H, step, 0)

        def clear(h, _):
            out[h] = jnp.zeros((W, CB, LANES), jnp.bfloat16)
            return 0
        lax.fori_loop(0, H, clear, 0)

        for k in range(1, TP):
            b_copy(k, tp).wait_send()

    w_sends(lambda c: c.wait_send())

    @pl.when(pp == 0)
    def _():
        for t in range(TP):
            for i in range(2):
                for q in range(2):
                    z_part(i, q, t, tp).wait_send()
            for h in list(range(1, G)) + list(range(H - G, LAST)):
                z_copy(h, 1, t, tp).wait_send()

        def drain(g, _):
            for t in range(TP):
                z_copy(g * G, G, t, tp).wait_send()
            return 0
        lax.fori_loop(1, GROUPS - 1, drain, 0)

    @pl.when(pp == 1)
    def _():
        def turn(h, first, count):
            for p in range(first, first + count):
                turned = buf[h, p].reshape(LANES, LANES).T
                out[h, p] = turned[:CB]
                out[h, p + PAIRS] = turned[CB:]

        def group(g, _):
            edge = jnp.logical_or(g == 0, g == GROUPS - 1)

            @pl.when(jnp.logical_not(edge))
            def _():
                for s in range(TP):
                    z_copy(g * G, G, s, s).wait_recv()

            def row(h, _):
                @pl.when(jnp.logical_and(edge, jnp.logical_and(h < LAST, h > 0)))
                def _():
                    for s in range(TP):
                        z_copy(h, 1, s, s).wait_recv()
                for q in range(2):
                    for i in range(2):
                        @pl.when(h == i * LAST)
                        def _():
                            for s in range(TP):
                                z_part(i, q, s, s).wait_recv()
                    turn(h, q * Q, Q)
                return 0
            lax.fori_loop(g * G, g * G + G, row, 0)
            return 0
        lax.fori_loop(0, GROUPS, group, 0)


def flush(src, dst, sem):
    rows = H // FLUSH
    copies = [pltpu.make_async_copy(src.at[pl.ds(i * rows, rows)], dst.at[pl.ds(i * rows, rows)], sem.at[i])
              for i in range(FLUSH)]
    for c in copies:
        c.start()
    for c in copies:
        c.wait()


def solution(mesh):
    def local_step(act, w, scale, shift):
        x = jnp.transpose(act, (1, 2, 0, 3))
        dma = pltpu.SemaphoreType.DMA
        shape = (H, W, CB, LANES)
        out = pl.pallas_call(
            kernel,
            out_shape=pltpu.VMEM(shape, jnp.bfloat16),
            in_specs=[pl.BlockSpec(memory_space=pl.ANY), pl.BlockSpec(memory_space=pl.ANY),
                      pl.BlockSpec(memory_space=pltpu.VMEM), pl.BlockSpec(memory_space=pltpu.VMEM)],
            out_specs=pl.BlockSpec(memory_space=pltpu.VMEM),
            scratch_shapes=[
                pltpu.VMEM((H + 2, W + 2, N_LOC, C), jnp.bfloat16),
                pltpu.VMEM((H, PAIRS, TP, N_LOC, LANES), jnp.bfloat16),
                pltpu.VMEM((2, 9, TP, C // TP, LANES), jnp.bfloat16),
                pltpu.VMEM((TP, 8, LANES), jnp.float32),
                dma((H,)), dma((2,)), dma((3, 3)), dma((3, TP)), dma((TP,)), dma((TP,)), dma((H, TP)), dma((H, TP)),
                dma((2, 2, TP)), dma((2, 2, TP)),
            ],
            compiler_params=pltpu.CompilerParams(collective_id=0, has_side_effects=True, vmem_limit_bytes=46 * 2**20),
        )(x, w.reshape(9, C // TP, C), scale.reshape(1, CB), shift.reshape(1, CB))
        out = pl.pallas_call(
            flush,
            out_shape=jax.ShapeDtypeStruct(shape, jnp.bfloat16),
            in_specs=[pl.BlockSpec(memory_space=pltpu.VMEM)],
            out_specs=pl.BlockSpec(memory_space=pl.ANY),
            scratch_shapes=[dma((FLUSH,))],
            compiler_params=pltpu.CompilerParams(vmem_limit_bytes=2**20),
        )(out)
        return jnp.transpose(out, (3, 0, 1, 2))

    return jax.shard_map(local_step, mesh=mesh, in_specs=(P(("pp", "tp")), P(None, None, "tp", None), P("tp"), P("tp")),
                         out_specs=P("pp", None, None, "tp"), check_vma=False)
```

time: 298 us -> 292 us (0.980)
  Pallas kernels: 296 us -> 292 us
    pallas_call x2, Pallas kernels: 296 us -> 292 us  [the longest x1 287 us: local_step(): pl.pallas_call(kernel, out_shape=pltpu.VMEM(shape, jnp.bfloat16), in_spec...]
where the time goes in v2:
time: 292 us
  Pallas kernels  292 us (100%)
    pallas_call x1, Pallas kernels, local_step(): pl.pallas_call(kernel, out_shape=pltpu.VMEM(shape, jnp.bfloat16), in_spec...  287 us

profile of v2, /device:TPU:1, one launch (start us, length us, event | category | flops | bytes accessed | tf_op | source)
XLA Modules:
  0.0 292.0 jit_solution(1769722384247293609)
XLA Ops:
  0.0 287.3 %shard_map.46.src = bf16[28,28,64,128]{3,2,1,0:T(8,128)(2,1)S(1)} custom-call(bf16[28,28,32,256]{3,2,1,0:T(8,128)(2,1)} %bitcast.5, bf16[9,64,256]{2,1,0:T(8,128)(2,1)} %bitcast.6, f32[1,64]{1,0:T(1,128)} %bitcast.7, f32[1,64]{1,0:T(1,128)} %bitcast.8), custom_call_target="tpu_custom_call" | custom-call | tf_op jit(solution)/shard_map/pallas_call | solution.py:266
  287.3 4.8 %shard_map.47 = bf16[28,28,64,128]{3,2,1,0:T(8,128)(2,1)} custom-call(bf16[28,28,64,128]{3,2,1,0:T(8,128)(2,1)S(1)} %shard_map.46.src), custom_call_target="tpu_custom_call" | custom-call | tf_op jit(solution)/shard_map/pallas_call | solution.py:282

commit v3 on v2

--- a/solution.py
+++ b/solution.py
@@ -16,11 +16,14 @@
 G = 4
 GROUPS = H // G
 LAST = H - 1
-FLUSH = 14
+FLUSH = 7
 PARTS = ((0, 3, 6), (0, 0, 3), (1, 0, 9))
-
-
-def kernel(act, w, scale, shift, out, xpad, buf, wf, sb, xsem, wlsem, wssem, wrsem, bssem, brsem, ssem, rsem, esem, fsem):
+EDGES = ((1, 1), (2, 2), (H - 4, 2), (H - 2, 1))
+EDGE_ROWS = 2
+ENDS = (((0, 7), (7, 7)), ((0, 4), (4, 8), (12, 2)))
+
+
+def kernel(act, w, scale, shift, out, xpad, buf, wf, sb, xsem, wlsem, wssem, wrsem, bssem, brsem, ssem, rsem, esem, fsem, vecs, vsem, ready):
     pp, tp = lax.axis_index("pp"), lax.axis_index("tp")
     chip, core = tp // 2, tp % 2
     far = 1 - chip
@@ -42,6 +45,9 @@
     def x_copy(h):
         return pltpu.make_async_copy(act.at[h], xpad.at[h + 1, pl.ds(1, W)], xsem.at[h])
 
+    def vec_copy(i):
+        return pltpu.make_async_copy((scale, shift)[i], vecs.at[i], vsem.at[i])
+
     def b_copy(k, owner):
         return pltpu.make_async_remote_copy(
             src_ref=sb.at[tp], dst_ref=sb.at[tp], send_sem=bssem.at[k], recv_sem=brsem.at[owner],
@@ -55,56 +61,88 @@
     def z_part(i, q, t, owner):
         h = 0 if i == 0 else LAST
         return pltpu.make_async_remote_copy(
-            src_ref=buf.at[h, pl.ds(q * Q, Q), t], dst_ref=buf.at[h, pl.ds(q * Q, Q), owner],
+            src_ref=buf.at[h, pl.ds(*ENDS[i][q]), t], dst_ref=buf.at[h, pl.ds(*ENDS[i][q]), owner],
             send_sem=esem.at[i, q, t], recv_sem=fsem.at[i, q, owner], device_id=(1, t), device_id_type=MESH)
 
-    sends_far = pp == core
-
-    @pl.when(jnp.logical_or(pp == 0, sends_far))
+    def middle_done(t):
+        def one(g, _):
+            z_copy(g * G, G, t, tp).wait_send()
+            return 0
+        lax.fori_loop(1, GROUPS - 1, one, 0)
+
+    barrier = pltpu.get_barrier_semaphore()
+
+    @pl.when(pp == 0)
+    def _():
+        for k in range(1, TP):
+            pl.semaphore_signal(barrier, inc=1, device_id=(0, lax.rem(tp + k, TP)), device_id_type=MESH)
+        for k in range(TP):
+            pl.semaphore_signal(barrier, inc=1, device_id=(1, lax.rem(tp + k, TP)), device_id_type=MESH)
+
+    helps = jnp.logical_and(pp == 1, core == 1)
+    has_w = jnp.logical_or(pp == 0, helps)
+
+    @pl.when(pp == 0)
+    def _():
+        vec_copy(0).start()
+        vec_copy(1).start()
+
+    @pl.when(has_w)
     def _():
         w_local(0).start()
         w_local(1).start()
 
     @pl.when(pp == 0)
     def _():
+        x_copy(0).start()
+        x_copy(1).start()
+        for i in range(2):
+            vec_copy(i).wait()
+            sb[tp, i : i + 1, :] = jnp.concatenate([vecs[i], vecs[i]], axis=1)
+
+    pl.semaphore_wait(barrier, TP - 1 + pp)
+
+    @pl.when(pp == 0)
+    def _():
+        for k in range(1, TP):
+            b_copy(k, tp).start()
+
+    @pl.when(has_w)
+    def _():
+        w_local(0).wait()
+        w_local(1).wait()
+
+    def w_sends(act_on):
+        for part, cores in ((0, (0,)), (0, (1,)), (1, (0, 1)), (2, (0, 1))):
+            near = part if cores[0] == 0 else None
+            sends = jnp.logical_or(jnp.logical_and(pp == 0, core == 0), helps)
+            if part == 0 and cores[0] == 0:
+                sends = pp == 0
+
+            @pl.when(sends)
+            def _():
+                for c in cores:
+                    act_on(w_copy(part, tp, c, far * 2 + c))
+
+            if near is not None:
+                @pl.when(pp == 0)
+                def _():
+                    act_on(w_copy(near, tp, 2, chip * 2 + 1 - core))
+
+    w_sends(lambda c: c.start())
+
+    @pl.when(pp == 1)
+    def _():
+        for k in range(TP):
+            pl.semaphore_signal(ready, inc=1, device_id=(0, lax.rem(tp + k, TP)), device_id_type=MESH)
+
+    @pl.when(pp == 0)
+    def _():
         def start_x(h, _):
             x_copy(h).start()
             return 0
-        lax.fori_loop(0, H, start_x, 0)
-        sb[tp, 0:1, :] = jnp.concatenate([scale[...], scale[...]], axis=1)
-        sb[tp, 1:2, :] = jnp.concatenate([shift[...], shift[...]], axis=1)
-
-    barrier = pltpu.get_barrier_semaphore()
-    for d in range(1, 2 * TP):
-        other = lax.rem(pp * TP + tp + d, 2 * TP)
-        pl.semaphore_signal(barrier, inc=1, device_id=(other // TP, other % TP), device_id_type=MESH)
-
-    @pl.when(jnp.logical_or(pp == 0, sends_far))
-    def _():
-        w_local(0).wait()
-        w_local(1).wait()
-    pl.semaphore_wait(barrier, 2 * TP - 1)
-
-    @pl.when(pp == 0)
-    def _():
-        for k in range(1, TP):
-            b_copy(k, tp).start()
-
-    def w_sends(act_on):
-        for part in range(len(PARTS)):
-            @pl.when(sends_far)
-            def _():
-                for c in range(2):
-                    act_on(w_copy(part, tp, c, far * 2 + c))
-
-            @pl.when(pp == 0)
-            def _():
-                act_on(w_copy(part, tp, 2, chip * 2 + 1 - core))
-
-    w_sends(lambda c: c.start())
-
-    @pl.when(pp == 0)
-    def _():
+        lax.fori_loop(2, H, start_x, 0)
+
         zero = jnp.zeros((W + 2, N_LOC, C), jnp.bfloat16)
         xpad[0] = zero
         xpad[H + 1] = zero
@@ -143,9 +181,16 @@
         wait_w(0)
         for q in range(2):
             pixels(0, chip, q, 3)
+            if q == 0:
+                pl.semaphore_wait(ready, TP)
             for k in range(2):
                 z_part(0, q, 2 * chip + k, tp).start()
         wait_w(1)
+
+        def last_sends(i, half, pieces):
+            for q in pieces:
+                for k in range(2):
+                    z_part(i, q, 2 * half + k, tp).start()
 
         def step(i, _):
             g, r = i // (2 * G), i % (2 * G)
@@ -164,25 +209,25 @@
             for q in range(2):
                 pixels(h, half, q, 0)
 
-                @pl.when(h == LAST)
+            @pl.when(h == 0)
+            def _():
+                last_sends(0, half, range(2))
+
+            for first, rows in EDGES:
+                @pl.when(h == first + rows - 1)
                 def _():
                     for k in range(2):
-                        z_part(1, q, 2 * half + k, tp).start()
-
-            edge = jnp.logical_or(g == 0, g == GROUPS - 1)
-
-            @pl.when(jnp.logical_and(edge, jnp.logical_and(h < LAST, h > 0)))
-            def _():
-                for k in range(2):
-                    z_copy(h, 1, 2 * half + k, tp).start()
-
-            @pl.when(h == 0)
-            def _():
-                for q in range(2):
-                    for k in range(2):
-                        z_part(0, q, 2 * half + k, tp).start()
-
-            @pl.when(jnp.logical_and(jnp.logical_not(edge), r % G == G - 1))
+                        z_copy(first, rows, 2 * half + k, tp).start()
+
+            @pl.when(h == LAST)
+            def _():
+                last_sends(1, half, range(1))
+
+            @pl.when(jnp.logical_and(h == LAST, jnp.logical_or(own, chip == 0)))
+            def _():
+                last_sends(1, half, range(1, 3))
+
+            @pl.when(jnp.logical_and(jnp.logical_and(g > 0, g < GROUPS - 1), r % G == G - 1))
             def _():
                 for k in range(2):
                     z_copy(g * G, G, 2 * half + k, tp).start()
@@ -194,6 +239,12 @@
             return 0
         lax.fori_loop(0, H, clear, 0)
 
+        @pl.when(chip == 1)
+        def _():
+            for k in range(2):
+                z_copy(*EDGES[-1], 2 * chip + k, tp).wait_send()
+            last_sends(1, far, range(1, 3))
+
         for k in range(1, TP):
             b_copy(k, tp).wait_send()
 
@@ -203,16 +254,18 @@
     def _():
         for t in range(TP):
             for i in range(2):
-                for q in range(2):
+                for q in range(len(ENDS[i])):
                     z_part(i, q, t, tp).wait_send()
-            for h in list(range(1, G)) + list(range(H - G, LAST)):
-                z_copy(h, 1, t, tp).wait_send()
-
-        def drain(g, _):
-            for t in range(TP):
-                z_copy(g * G, G, t, tp).wait_send()
-            return 0
-        lax.fori_loop(1, GROUPS - 1, drain, 0)
+            for first, rows in EDGES[:-1]:
+                z_copy(first, rows, t, tp).wait_send()
+            middle_done(t)
+        for k in range(2):
+            z_copy(*EDGES[-1], 2 * far + k, tp).wait_send()
+
+        @pl.when(chip == 0)
+        def _():
+            for k in range(2):
+                z_copy(*EDGES[-1], 2 * chip + k, tp).wait_send()
 
     @pl.when(pp == 1)
     def _():
@@ -222,30 +275,36 @@
                 out[h, p] = turned[:CB]
                 out[h, p + PAIRS] = turned[CB:]
 
+        def arrived(first, rows):
+            for s in range(TP):
+                z_copy(first, rows, s, s).wait_recv()
+
+        def turn_rows(first, rows):
+            def row(h, _):
+                turn(h, 0, PAIRS)
+                return 0
+            lax.fori_loop(first, first + rows, row, 0)
+
+        def end(i):
+            for q in range(len(ENDS[i])):
+                for s in range(TP):
+                    z_part(i, q, s, s).wait_recv()
+                turn(i * LAST, *ENDS[i][q])
+
+        end(0)
+        for first, rows in EDGES[:EDGE_ROWS]:
+            arrived(first, rows)
+            turn_rows(first, rows)
+
         def group(g, _):
-            edge = jnp.logical_or(g == 0, g == GROUPS - 1)
-
-            @pl.when(jnp.logical_not(edge))
-            def _():
-                for s in range(TP):
-                    z_copy(g * G, G, s, s).wait_recv()
-
-            def row(h, _):
-                @pl.when(jnp.logical_and(edge, jnp.logical_and(h < LAST, h > 0)))
-                def _():
-                    for s in range(TP):
-                        z_copy(h, 1, s, s).wait_recv()
-                for q in range(2):
-                    for i in range(2):
-                        @pl.when(h == i * LAST)
-                        def _():
-                            for s in range(TP):
-                                z_part(i, q, s, s).wait_recv()
-                    turn(h, q * Q, Q)
-                return 0
-            lax.fori_loop(g * G, g * G + G, row, 0)
-            return 0
-        lax.fori_loop(0, GROUPS, group, 0)
+            arrived(g * G, G)
+            turn_rows(g * G, G)
+            return 0
+        lax.fori_loop(1, GROUPS - 1, group, 0)
+        for first, rows in EDGES[EDGE_ROWS:]:
+            arrived(first, rows)
+            turn_rows(first, rows)
+        end(1)
 
 
 def flush(src, dst, sem):
@@ -267,7 +326,7 @@
             kernel,
             out_shape=pltpu.VMEM(shape, jnp.bfloat16),
             in_specs=[pl.BlockSpec(memory_space=pl.ANY), pl.BlockSpec(memory_space=pl.ANY),
-                      pl.BlockSpec(memory_space=pltpu.VMEM), pl.BlockSpec(memory_space=pltpu.VMEM)],
+                      pl.BlockSpec(memory_space=pl.ANY), pl.BlockSpec(memory_space=pl.ANY)],
             out_specs=pl.BlockSpec(memory_space=pltpu.VMEM),
             scratch_shapes=[
                 pltpu.VMEM((H + 2, W + 2, N_LOC, C), jnp.bfloat16),
@@ -275,7 +334,7 @@
                 pltpu.VMEM((2, 9, TP, C // TP, LANES), jnp.bfloat16),
                 pltpu.VMEM((TP, 8, LANES), jnp.float32),
                 dma((H,)), dma((2,)), dma((3, 3)), dma((3, TP)), dma((TP,)), dma((TP,)), dma((H, TP)), dma((H, TP)),
-                dma((2, 2, TP)), dma((2, 2, TP)),
+                dma((2, 3, TP)), dma((2, 3, TP)), pltpu.VMEM((2, 1, CB), jnp.float32), dma((2,)), pltpu.SemaphoreType.REGULAR,
             ],
             compiler_params=pltpu.CompilerParams(collective_id=0, has_side_effects=True, vmem_limit_bytes=46 * 2**20),
         )(x, w.reshape(9, C // TP, C), scale.reshape(1, CB), shift.reshape(1, CB))

time: 292 us -> 291 us (level); the launches traced: 292 us -> 288 us
  Pallas kernels: 292 us -> 288 us
    pallas_call x1, Pallas kernels: 287 us -> 283 us  [local_step(): pl.pallas_call(kernel, out_shape=pltpu.VMEM(shape, jnp.bfloat16), in_spec...]
where the time goes in v3:
time: 291 us; the launch traced here: 288 us
  Pallas kernels  288 us (99%)
    pallas_call x1, Pallas kernels, local_step(): pl.pallas_call(kernel, out_shape=pltpu.VMEM(shape, jnp.bfloat16), in_spec...  283 us

profile of v3, /device:TPU:1, one launch (start us, length us, event | category | flops | bytes accessed | tf_op | source)
XLA Modules:
  0.0 287.7 jit_solution(1107091611576406909)
XLA Ops:
  0.0 282.9 %shard_map.46.src = bf16[28,28,64,128]{3,2,1,0:T(8,128)(2,1)S(1)} custom-call(bf16[28,28,32,256]{3,2,1,0:T(8,128)(2,1)} %bitcast.5, bf16[9,64,256]{2,1,0:T(8,128)(2,1)} %bitcast.6, f32[1,64]{1,0:T(1,128)} %bitcast.7, f32[1,64]{1,0:T(1,128)} %bitcast.8), custom_call_target="tpu_custom_call" | custom-call | tf_op jit(solution)/shard_map/pallas_call | solution.py:325
  283.0 4.8 %shard_map.47 = bf16[28,28,64,128]{3,2,1,0:T(8,128)(2,1)} custom-call(bf16[28,28,64,128]{3,2,1,0:T(8,128)(2,1)S(1)} %shard_map.46.src), custom_call_target="tpu_custom_call" | custom-call | tf_op jit(solution)/shard_map/pallas_call | solution.py:341

commit v4 on v3

--- a/solution.py
+++ b/solution.py
@@ -17,9 +17,12 @@
 GROUPS = H // G
 LAST = H - 1
 FLUSH = 7
-PARTS = ((0, 3, 6), (0, 0, 3), (1, 0, 9))
+PARTS = ((0, 3, 3), (0, 6, 3), (0, 0, 3), (1, 0, 9))
+ORDER = (1, 0)
 EDGES = ((1, 1), (2, 2), (H - 4, 2), (H - 2, 1))
 EDGE_ROWS = 2
+FIRST = ((0, 0), (1, 0), (0, 1), (1, 1))
+REST = ((2, 0), (2, 1), (3, 0), (3, 1))
 ENDS = (((0, 7), (7, 7)), ((0, 4), (4, 8), (12, 2)))
 
 
@@ -102,6 +105,11 @@
 
     pl.semaphore_wait(barrier, TP - 1 + pp)
 
+    @pl.when(pp == 1)
+    def _():
+        for k in range(TP):
+            pl.semaphore_signal(ready, inc=1, device_id=(0, lax.rem(tp + k, TP)), device_id_type=MESH)
+
     @pl.when(pp == 0)
     def _():
         for k in range(1, TP):
@@ -112,29 +120,26 @@
         w_local(0).wait()
         w_local(1).wait()
 
-    def w_sends(act_on):
-        for part, cores in ((0, (0,)), (0, (1,)), (1, (0, 1)), (2, (0, 1))):
-            near = part if cores[0] == 0 else None
+    def w_sends(act_on, stages):
+        for part, c in stages:
             sends = jnp.logical_or(jnp.logical_and(pp == 0, core == 0), helps)
-            if part == 0 and cores[0] == 0:
+            if (part, c) == FIRST[0]:
                 sends = pp == 0
 
             @pl.when(sends)
             def _():
-                for c in cores:
-                    act_on(w_copy(part, tp, c, far * 2 + c))
-
-            if near is not None:
+                act_on(w_copy(part, tp, c, far * 2 + c))
+
+            if c == 0:
                 @pl.when(pp == 0)
                 def _():
-                    act_on(w_copy(near, tp, 2, chip * 2 + 1 - core))
-
-    w_sends(lambda c: c.start())
+                    act_on(w_copy(part, tp, 2, chip * 2 + 1 - core))
+
+    w_sends(lambda c: c.start(), FIRST)
 
     @pl.when(pp == 1)
     def _():
-        for k in range(TP):
-            pl.semaphore_signal(ready, inc=1, device_id=(0, lax.rem(tp + k, TP)), device_id_type=MESH)
+        w_sends(lambda c: c.start(), REST)
 
     @pl.when(pp == 0)
     def _():
@@ -158,39 +163,41 @@
             for k in range(1, TP):
                 w_copy(part, lax.rem(tp + k, TP), 0, tp).wait_recv()
 
-        def pixels(h, half, q, first_tap):
+        def pixels(h, half, start, count, first_tap):
             sc = jnp.where(low, sb[2 * half, 0:1, :], sb[2 * half + 1, 0:1, :])
             sh = jnp.where(low, sb[2 * half, 1:2, :], sb[2 * half + 1, 1:2, :])
 
             def conv(w0):
                 acc = None
                 for tap in range(first_tap, 9):
-                    lhs = xpad[h + tap // 3, pl.ds(w0 + tap % 3, Q)].reshape(Q * N_LOC, C)
+                    lhs = xpad[h + tap // 3, pl.ds(w0 + tap % 3, count)].reshape(count * N_LOC, C)
                     part = jnp.dot(lhs, wf[half, tap].reshape(C, LANES), preferred_element_type=jnp.float32)
                     acc = part if acc is None else acc + part
                 return jnp.maximum(acc * sc + sh, 0.0)
 
-            even, odd = conv(q * Q), conv(PAIRS + q * Q)
+            even, odd = conv(start), conv(PAIRS + start)
             first = jnp.where(low, even, pltpu.roll(odd, CB, 1)).astype(jnp.bfloat16)
             second = jnp.where(low, pltpu.roll(even, CB, 1), odd).astype(jnp.bfloat16)
-            buf[h, pl.ds(q * Q, Q), 2 * half] = first.reshape(Q, N_LOC, LANES)
-            buf[h, pl.ds(q * Q, Q), 2 * half + 1] = second.reshape(Q, N_LOC, LANES)
+            buf[h, pl.ds(start, count), 2 * half] = first.reshape(count, N_LOC, LANES)
+            buf[h, pl.ds(start, count), 2 * half + 1] = second.reshape(count, N_LOC, LANES)
 
         x_copy(0).wait()
         x_copy(1).wait()
         wait_w(0)
-        for q in range(2):
-            pixels(0, chip, q, 3)
+        wait_w(1)
+        for q, (start, count) in enumerate(ENDS[0]):
+            pixels(0, chip, start, count, 3)
             if q == 0:
                 pl.semaphore_wait(ready, TP)
-            for k in range(2):
+            for k in ORDER:
                 z_part(0, q, 2 * chip + k, tp).start()
-        wait_w(1)
-
-        def last_sends(i, half, pieces):
+        w_sends(lambda c: c.start(), REST)
+        wait_w(2)
+
+        def last_sends(half, pieces):
             for q in pieces:
-                for k in range(2):
-                    z_part(i, q, 2 * half + k, tp).start()
+                for k in ORDER:
+                    z_part(1, q, 2 * half + k, tp).start()
 
         def step(i, _):
             g, r = i // (2 * G), i % (2 * G)
@@ -200,36 +207,37 @@
 
             @pl.when(i == G)
             def _():
-                wait_w(2)
+                wait_w(3)
 
             @pl.when(jnp.logical_and(own, h < LAST))
             def _():
                 x_copy(h + 1).wait()
 
             for q in range(2):
-                pixels(h, half, q, 0)
+                pixels(h, half, q * Q, Q, 0)
 
             @pl.when(h == 0)
             def _():
-                last_sends(0, half, range(2))
+                for k in ORDER:
+                    z_copy(0, 1, 2 * half + k, tp).start()
 
             for first, rows in EDGES:
                 @pl.when(h == first + rows - 1)
                 def _():
-                    for k in range(2):
+                    for k in ORDER:
                         z_copy(first, rows, 2 * half + k, tp).start()
 
             @pl.when(h == LAST)
             def _():
-                last_sends(1, half, range(1))
+                last_sends(half, range(1))
 
             @pl.when(jnp.logical_and(h == LAST, jnp.logical_or(own, chip == 0)))
             def _():
-                last_sends(1, half, range(1, 3))
+                last_sends(half, range(1, 3))
 
             @pl.when(jnp.logical_and(jnp.logical_and(g > 0, g < GROUPS - 1), r % G == G - 1))
             def _():
-                for k in range(2):
+                for k in ORDER:
                     z_copy(g * G, G, 2 * half + k, tp).start()
             return 0
         lax.fori_loop(1, 2 * H, step, 0)
@@ -243,23 +251,25 @@
         def _():
             for k in range(2):
                 z_copy(*EDGES[-1], 2 * chip + k, tp).wait_send()
-            last_sends(1, far, range(1, 3))
+            last_sends(far, range(1, 3))
 
         for k in range(1, TP):
             b_copy(k, tp).wait_send()
 
-    w_sends(lambda c: c.wait_send())
+    w_sends(lambda c: c.wait_send(), FIRST + REST)
 
     @pl.when(pp == 0)
     def _():
         for t in range(TP):
-            for i in range(2):
-                for q in range(len(ENDS[i])):
-                    z_part(i, q, t, tp).wait_send()
+            for q in range(len(ENDS[1])):
+                z_part(1, q, t, tp).wait_send()
             for first, rows in EDGES[:-1]:
                 z_copy(first, rows, t, tp).wait_send()
             middle_done(t)
         for k in range(2):
+            for q in range(len(ENDS[0])):
+                z_part(0, q, 2 * chip + k, tp).wait_send()
+            z_copy(0, 1, 2 * far + k, tp).wait_send()
             z_copy(*EDGES[-1], 2 * far + k, tp).wait_send()
 
         @pl.when(chip == 0)
@@ -285,13 +295,11 @@
                 return 0
             lax.fori_loop(first, first + rows, row, 0)
 
-        def end(i):
-            for q in range(len(ENDS[i])):
-                for s in range(TP):
-                    z_part(i, q, s, s).wait_recv()
-                turn(i * LAST, *ENDS[i][q])
-
-        end(0)
+        for k in range(2):
+            for q in range(len(ENDS[0])):
+                z_part(0, q, 2 * chip + k, 2 * chip + k).wait_recv()
+            z_copy(0, 1, 2 * far + k, 2 * far + k).wait_recv()
+        turn(0, 0, PAIRS)
         for first, rows in EDGES[:EDGE_ROWS]:
             arrived(first, rows)
             turn_rows(first, rows)
@@ -304,7 +312,10 @@
         for first, rows in EDGES[EDGE_ROWS:]:
             arrived(first, rows)
             turn_rows(first, rows)
-        end(1)
+        for q in range(len(ENDS[1])):
+            for s in range(TP):
+                z_part(1, q, s, s).wait_recv()
+            turn(LAST, *ENDS[1][q])
 
 
 def flush(src, dst, sem):
@@ -333,7 +344,7 @@
                 pltpu.VMEM((H, PAIRS, TP, N_LOC, LANES), jnp.bfloat16),
                 pltpu.VMEM((2, 9, TP, C // TP, LANES), jnp.bfloat16),
                 pltpu.VMEM((TP, 8, LANES), jnp.float32),
-                dma((H,)), dma((2,)), dma((3, 3)), dma((3, TP)), dma((TP,)), dma((TP,)), dma((H, TP)), dma((H, TP)),
+                dma((H,)), dma((2,)), dma((4, 3)), dma((4, TP)), dma((TP,)), dma((TP,)), dma((H, TP)), dma((H, TP)),
                 dma((2, 3, TP)), dma((2, 3, TP)), pltpu.VMEM((2, 1, CB), jnp.float32), dma((2,)), pltpu.SemaphoreType.REGULAR,
             ],
             compiler_params=pltpu.CompilerParams(collective_id=0, has_side_effects=True, vmem_limit_bytes=46 * 2**20),

time: 291 us -> 291 us (level)
  no operation moved by 1% of the time
where the time goes in v4:
time: 291 us; the launch traced here: 287 us
  Pallas kernels  287 us (99%)
    pallas_call x1, Pallas kernels, local_step(): pl.pallas_call(kernel, out_shape=pltpu.VMEM(shape, jnp.bfloat16), in_spec...  282 us

profile of v4, /device:TPU:1, one launch (start us, length us, event | category | flops | bytes accessed | tf_op | source)
XLA Modules:
  0.0 287.1 jit_solution(6082257797918536826)
XLA Ops:
  0.0 282.3 %shard_map.46.src = bf16[28,28,64,128]{3,2,1,0:T(8,128)(2,1)S(1)} custom-call(bf16[28,28,32,256]{3,2,1,0:T(8,128)(2,1)} %bitcast.5, bf16[9,64,256]{2,1,0:T(8,128)(2,1)} %bitcast.6, f32[1,64]{1,0:T(1,128)} %bitcast.7, f32[1,64]{1,0:T(1,128)} %bitcast.8), custom_call_target="tpu_custom_call" | custom-call | tf_op jit(solution)/shard_map/pallas_call | solution.py:336
  282.4 4.8 %shard_map.47 = bf16[28,28,64,128]{3,2,1,0:T(8,128)(2,1)} custom-call(bf16[28,28,64,128]{3,2,1,0:T(8,128)(2,1)S(1)} %shard_map.46.src), custom_call_target="tpu_custom_call" | custom-call | tf_op jit(solution)/shard_map/pallas_call | solution.py:352

commit v5 on v4

--- a/solution.py
+++ b/solution.py
@@ -1,3 +1,5 @@
+import functools
+
 import jax
 import jax.numpy as jnp
 from jax import lax
@@ -16,17 +18,22 @@
 G = 4
 GROUPS = H // G
 LAST = H - 1
-FLUSH = 7
+SPLIT = 20
+ODD_SPLIT = 24
+LATE = H - SPLIT
 PARTS = ((0, 3, 3), (0, 6, 3), (0, 0, 3), (1, 0, 9))
 ORDER = (1, 0)
-EDGES = ((1, 1), (2, 2), (H - 4, 2), (H - 2, 1))
-EDGE_ROWS = 2
 FIRST = ((0, 0), (1, 0), (0, 1), (1, 1))
 REST = ((2, 0), (2, 1), (3, 0), (3, 1))
-ENDS = (((0, 7), (7, 7)), ((0, 4), (4, 8), (12, 2)))
-
-
-def kernel(act, w, scale, shift, out, xpad, buf, wf, sb, xsem, wlsem, wssem, wrsem, bssem, brsem, ssem, rsem, esem, fsem, vecs, vsem, ready):
+HEAD = ((0, 7), (7, 7))
+ROWS = ((1, 1), (2, 2), (4, 4), (8, 8), (16, 4))
+ODD_ROWS = (SPLIT, ODD_SPLIT - SPLIT)
+LATE_EVEN = ((0, 4), (4, 2), (6, 1))
+LATE_ODD = ((4, 2), (6, 1))
+TAIL = ((0, 7), (7, 5), (12, 2))
+
+
+def kernel(act, w, scale, shift, out, buf, xpad, wf, sb, xsem, wlsem, wssem, wrsem, bssem, brsem, ssem, rsem, esem, fsem, vecs, vsem, ready):
     pp, tp = lax.axis_index("pp"), lax.axis_index("tp")
     chip, core = tp // 2, tp % 2
     far = 1 - chip
@@ -61,17 +68,10 @@
             src_ref=buf.at[pl.ds(h, rows), :, t], dst_ref=buf.at[pl.ds(h, rows), :, owner],
             send_sem=ssem.at[h, t], recv_sem=rsem.at[h, owner], device_id=(1, t), device_id_type=MESH)
 
-    def z_part(i, q, t, owner):
-        h = 0 if i == 0 else LAST
-        return pltpu.make_async_remote_copy(
-            src_ref=buf.at[h, pl.ds(*ENDS[i][q]), t], dst_ref=buf.at[h, pl.ds(*ENDS[i][q]), owner],
-            send_sem=esem.at[i, q, t], recv_sem=fsem.at[i, q, owner], device_id=(1, t), device_id_type=MESH)
-
-    def middle_done(t):
-        def one(g, _):
-            z_copy(g * G, G, t, tp).wait_send()
-            return 0
-        lax.fori_loop(1, GROUPS - 1, one, 0)
+    def z_head(q, t, owner):
+        return pltpu.make_async_remote_copy(
+            src_ref=buf.at[0, pl.ds(*HEAD[q]), t], dst_ref=buf.at[0, pl.ds(*HEAD[q]), owner],
+            send_sem=esem.at[q, t], recv_sem=fsem.at[q, owner], device_id=(1, t), device_id_type=MESH)
 
     barrier = pltpu.get_barrier_semaphore()
 
@@ -185,19 +185,14 @@
         x_copy(1).wait()
         wait_w(0)
         wait_w(1)
-        for q, (start, count) in enumerate(ENDS[0]):
+        for q, (start, count) in enumerate(HEAD):
             pixels(0, chip, start, count, 3)
             if q == 0:
                 pl.semaphore_wait(ready, TP)
             for k in ORDER:
-                z_part(0, q, 2 * chip + k, tp).start()
+                z_head(q, 2 * chip + k, tp).start()
         w_sends(lambda c: c.start(), REST)
         wait_w(2)
-
-        def last_sends(half, pieces):
-            for q in pieces:
-                for k in ORDER:
-                    z_part(1, q, 2 * half + k, tp).start()
 
         def step(i, _):
             g, r = i // (2 * G), i % (2 * G)
@@ -216,42 +211,47 @@
             for q in range(2):
                 pixels(h, half, q * Q, Q, 0)
 
+            def send(first, rows, cores):
+                for k in cores:
+                    z_copy(first, rows, 2 * half + k, tp).start()
+
             @pl.when(h == 0)
             def _():
-                for k in ORDER:
-                    z_copy(0, 1, 2 * half + k, tp).start()
-
-            for first, rows in EDGES:
+                send(0, 1, (0, 1))
+
+            for first, rows in ROWS[:-1]:
                 @pl.when(h == first + rows - 1)
                 def _():
-                    for k in ORDER:
-                        z_copy(first, rows, 2 * half + k, tp).start()
-
-            @pl.when(h == LAST)
-            def _():
-                last_sends(half, range(1))
-
-            @pl.when(jnp.logical_and(h == LAST, jnp.logical_or(own, chip == 0)))
-            def _():
-                last_sends(half, range(1, 3))
-
-            @pl.when(jnp.logical_and(jnp.logical_and(g > 0, g < GROUPS - 1), r % G == G - 1))
-            def _():
-                for k in ORDER:
-                    z_copy(g * G, G, 2 * half + k, tp).start()
+                    send(first, rows, (0, 1))
+
+            last = jnp.logical_and(own, core == 1)
+
+            @pl.when(h == SPLIT - 1)
+            def _():
+                send(*ROWS[-1], (0,))
+
+            @pl.when(jnp.logical_and(h == SPLIT - 1, jnp.logical_not(last)))
+            def _():
+                send(*ROWS[-1], (1,))
+
+            @pl.when(jnp.logical_and(h == ODD_SPLIT - 1, core == 1))
+            def _():
+                send(*ODD_ROWS, (0,))
+
+            @pl.when(jnp.logical_and(h == ODD_SPLIT - 1, last))
+            def _():
+                send(*ROWS[-1], (1,))
+
+            @pl.when(jnp.logical_and(h == ODD_SPLIT - 1, core == 1))
+            def _():
+                send(*ODD_ROWS, (1,))
             return 0
         lax.fori_loop(1, 2 * H, step, 0)
 
         def clear(h, _):
             out[h] = jnp.zeros((W, CB, LANES), jnp.bfloat16)
             return 0
-        lax.fori_loop(0, H, clear, 0)
-
-        @pl.when(chip == 1)
-        def _():
-            for k in range(2):
-                z_copy(*EDGES[-1], 2 * chip + k, tp).wait_send()
-            last_sends(far, range(1, 3))
+        lax.fori_loop(0, SPLIT, clear, 0)
 
         for k in range(1, TP):
             b_copy(k, tp).wait_send()
@@ -260,68 +260,150 @@
 
     @pl.when(pp == 0)
     def _():
+        for k in range(2):
+            for q in range(len(HEAD)):
+                z_head(q, 2 * chip + k, tp).wait_send()
+            z_copy(0, 1, 2 * far + k, tp).wait_send()
         for t in range(TP):
-            for q in range(len(ENDS[1])):
-                z_part(1, q, t, tp).wait_send()
-            for first, rows in EDGES[:-1]:
+            for first, rows in ROWS:
                 z_copy(first, rows, t, tp).wait_send()
-            middle_done(t)
+
+            @pl.when(core == 1)
+            def _():
+                z_copy(*ODD_ROWS, t, tp).wait_send()
+
+    @pl.when(pp == 1)
+    def _():
+        def turn_rows(first, rows):
+            def row(h, _):
+                for p in range(PAIRS):
+                    turn(buf[h, p].reshape(LANES, LANES), out, h, p)
+                return 0
+            lax.fori_loop(first, first + rows, row, 0)
+
         for k in range(2):
-            for q in range(len(ENDS[0])):
-                z_part(0, q, 2 * chip + k, tp).wait_send()
-            z_copy(0, 1, 2 * far + k, tp).wait_send()
-            z_copy(*EDGES[-1], 2 * far + k, tp).wait_send()
-
-        @pl.when(chip == 0)
-        def _():
-            for k in range(2):
-                z_copy(*EDGES[-1], 2 * chip + k, tp).wait_send()
-
-    @pl.when(pp == 1)
-    def _():
-        def turn(h, first, count):
-            for p in range(first, first + count):
-                turned = buf[h, p].reshape(LANES, LANES).T
-                out[h, p] = turned[:CB]
-                out[h, p + PAIRS] = turned[CB:]
-
-        def arrived(first, rows):
+            for q in range(len(HEAD)):
+                z_head(q, 2 * chip + k, 2 * chip + k).wait_recv()
+            z_copy(0, 1, 2 * far + k, 2 * far + k).wait_recv()
+        turn_rows(0, 1)
+        for first, rows in ROWS:
             for s in range(TP):
                 z_copy(first, rows, s, s).wait_recv()
-
-        def turn_rows(first, rows):
+            turn_rows(first, rows)
+        for s in (1, 3):
+            z_copy(*ODD_ROWS, s, s).wait_recv()
+
+
+def turn(block, out, h, p):
+    turned = block.T
+    out[h, p] = turned[:CB]
+    out[h, p + PAIRS] = turned[CB:]
+
+
+def finish(z, _, out, got, ssem, rsem, tsem, usem, ready):
+    pp, tp = lax.axis_index("pp"), lax.axis_index("tp")
+    core = tp % 2
+    source = pp == 0
+    even = core == 0
+
+    def z_copy(first, rows, t, owner):
+        return pltpu.make_async_remote_copy(
+            src_ref=z.at[pl.ds(SPLIT + first, rows), :, t], dst_ref=got.at[pl.ds(first, rows), :, owner],
+            send_sem=ssem.at[first, t], recv_sem=rsem.at[first, owner], device_id=(1, t), device_id_type=MESH)
+
+    def z_tail(q, t, owner):
+        return pltpu.make_async_remote_copy(
+            src_ref=z.at[LAST, pl.ds(*TAIL[q]), t], dst_ref=got.at[LATE - 1, pl.ds(*TAIL[q]), owner],
+            send_sem=tsem.at[q, t], recv_sem=usem.at[q, owner], device_id=(1, t), device_id_type=MESH)
+
+    def copies(rows, t, owner):
+        return [z_copy(*r, t, owner) for r in rows] + [z_tail(q, t, owner) for q in range(len(TAIL))]
+
+    barrier = pltpu.get_barrier_semaphore()
+
+    def greet(where, targets):
+        @pl.when(where)
+        def _():
+            for target in targets:
+                pl.semaphore_signal(barrier, inc=1, device_id=target, device_id_type=MESH)
+
+    greet(source & even, [(1, 0), (1, 2), (1, 1), (1, 3), (0, lax.rem(tp + 2, TP))])
+    greet(source & ~even, [(1, 1), (1, 3)])
+    greet(~source & even, [(0, 1), (0, 3)])
+    pl.semaphore_wait(barrier, jnp.where(source, jnp.where(even, 1, 2), jnp.where(even, 2, 4)))
+
+    @pl.when(~source & even)
+    def _():
+        for t in (0, 2):
+            pl.semaphore_signal(ready.at[0], inc=1, device_id=(0, t), device_id_type=MESH)
+
+    @pl.when(~source & ~even)
+    def _():
+        for t in range(TP):
+            pl.semaphore_signal(ready.at[1], inc=1, device_id=(0, t), device_id_type=MESH)
+
+    def sends(rows, k):
+        for a in zip(*[copies(rows, t, tp) for t in (k, 2 + k)]):
+            for c in a:
+                c.start()
+
+    @pl.when(source & even)
+    def _():
+        pl.semaphore_wait(ready.at[0], 2)
+        sends(LATE_EVEN, 0)
+        pl.semaphore_wait(ready.at[1], 2)
+        sends(LATE_EVEN, 1)
+
+    @pl.when(source & ~even)
+    def _():
+        sends(LATE_ODD, 0)
+        pl.semaphore_wait(ready.at[1], 2)
+        sends(LATE_ODD, 1)
+
+    @pl.when(source)
+    def _():
+        def clear(h, _):
+            out[h] = jnp.zeros((W, CB, LANES), jnp.bfloat16)
+            return 0
+        lax.fori_loop(0, LATE, clear, 0)
+        for rows, where in ((LATE_EVEN, even), (LATE_ODD, ~even)):
+            @pl.when(where)
+            def _():
+                for t in range(TP):
+                    for c in copies(rows, t, tp):
+                        c.wait_send()
+
+    @pl.when(~source)
+    def _():
+        for s in (0, 2):
+            z_copy(*LATE_EVEN[0], s, s).wait_recv()
+
+        def mixed(h, _):
+            for p in range(PAIRS):
+                parts = [got[h, p, s] if s % 2 == 0 else z[SPLIT + h, p, s] for s in range(TP)]
+                turn(jnp.concatenate(parts, axis=0), out, h, p)
+            return 0
+        lax.fori_loop(0, ODD_SPLIT - SPLIT, mixed, 0)
+        for first, rows in LATE_ODD:
+            for s in range(TP):
+                z_copy(first, rows, s, s).wait_recv()
+
             def row(h, _):
-                turn(h, 0, PAIRS)
+                for p in range(PAIRS):
+                    turn(got[h, p].reshape(LANES, LANES), out, h, p)
                 return 0
             lax.fori_loop(first, first + rows, row, 0)
-
-        for k in range(2):
-            for q in range(len(ENDS[0])):
-                z_part(0, q, 2 * chip + k, 2 * chip + k).wait_recv()
-            z_copy(0, 1, 2 * far + k, 2 * far + k).wait_recv()
-        turn(0, 0, PAIRS)
-        for first, rows in EDGES[:EDGE_ROWS]:
-            arrived(first, rows)
-            turn_rows(first, rows)
-
-        def group(g, _):
-            arrived(g * G, G)
-            turn_rows(g * G, G)
-            return 0
-        lax.fori_loop(1, GROUPS - 1, group, 0)
-        for first, rows in EDGES[EDGE_ROWS:]:
-            arrived(first, rows)
-            turn_rows(first, rows)
-        for q in range(len(ENDS[1])):
+        for q, (start, count) in enumerate(TAIL):
             for s in range(TP):
-                z_part(1, q, s, s).wait_recv()
-            turn(LAST, *ENDS[1][q])
-
-
-def flush(src, dst, sem):
-    rows = H // FLUSH
-    copies = [pltpu.make_async_copy(src.at[pl.ds(i * rows, rows)], dst.at[pl.ds(i * rows, rows)], sem.at[i])
-              for i in range(FLUSH)]
+                z_tail(q, s, s).wait_recv()
+            for p in range(start, start + count):
+                turn(got[LATE - 1, p].reshape(LANES, LANES), out, LATE - 1, p)
+
+
+def write(first, rows, each, src, *refs):
+    dst, _, sem = refs[-3:]
+    copies = [pltpu.make_async_copy(src.at[pl.ds(i * each, each)], dst.at[pl.ds(first + i * each, each)], sem.at[i])
+              for i in range(rows // each)]
     for c in copies:
         c.start()
     for c in copies:
@@ -333,30 +415,40 @@
         x = jnp.transpose(act, (1, 2, 0, 3))
         dma = pltpu.SemaphoreType.DMA
         shape = (H, W, CB, LANES)
-        out = pl.pallas_call(
+        vmem, hbm = pl.BlockSpec(memory_space=pltpu.VMEM), pl.BlockSpec(memory_space=pl.ANY)
+        early, z = pl.pallas_call(
             kernel,
-            out_shape=pltpu.VMEM(shape, jnp.bfloat16),
+            out_shape=(pltpu.VMEM((SPLIT, W, CB, LANES), jnp.bfloat16),
+                       pltpu.VMEM((H, PAIRS, TP, N_LOC, LANES), jnp.bfloat16)),
             in_specs=[pl.BlockSpec(memory_space=pl.ANY), pl.BlockSpec(memory_space=pl.ANY),
                       pl.BlockSpec(memory_space=pl.ANY), pl.BlockSpec(memory_space=pl.ANY)],
-            out_specs=pl.BlockSpec(memory_space=pltpu.VMEM),
+            out_specs=(vmem, vmem),
             scratch_shapes=[
                 pltpu.VMEM((H + 2, W + 2, N_LOC, C), jnp.bfloat16),
-                pltpu.VMEM((H, PAIRS, TP, N_LOC, LANES), jnp.bfloat16),
                 pltpu.VMEM((2, 9, TP, C // TP, LANES), jnp.bfloat16),
                 pltpu.VMEM((TP, 8, LANES), jnp.float32),
                 dma((H,)), dma((2,)), dma((4, 3)), dma((4, TP)), dma((TP,)), dma((TP,)), dma((H, TP)), dma((H, TP)),
-                dma((2, 3, TP)), dma((2, 3, TP)), pltpu.VMEM((2, 1, CB), jnp.float32), dma((2,)), pltpu.SemaphoreType.REGULAR,
+                dma((2, TP)), dma((2, TP)), pltpu.VMEM((2, 1, CB), jnp.float32), dma((2,)), pltpu.SemaphoreType.REGULAR,
             ],
-            compiler_params=pltpu.CompilerParams(collective_id=0, has_side_effects=True, vmem_limit_bytes=46 * 2**20),
+            compiler_params=pltpu.CompilerParams(collective_id=0, has_side_effects=True, vmem_limit_bytes=44040192),
         )(x, w.reshape(9, C // TP, C), scale.reshape(1, CB), shift.reshape(1, CB))
-        out = pl.pallas_call(
-            flush,
-            out_shape=jax.ShapeDtypeStruct(shape, jnp.bfloat16),
-            in_specs=[pl.BlockSpec(memory_space=pltpu.VMEM)],
-            out_specs=pl.BlockSpec(memory_space=pl.ANY),
-            scratch_shapes=[dma((FLUSH,))],
-            compiler_params=pltpu.CompilerParams(vmem_limit_bytes=2**20),
-        )(out)
+        small = pltpu.CompilerParams(vmem_limit_bytes=2**20)
+        written = (jax.ShapeDtypeStruct(shape, jnp.bfloat16), jax.ShapeDtypeStruct((8, LANES), jnp.float32))
+        out, token = pl.pallas_call(
+            functools.partial(write, 0, SPLIT, 4), out_shape=written, in_specs=[vmem], out_specs=(hbm, hbm), scratch_shapes=[dma((SPLIT // 4,))], compiler_params=small)(early)
+        late = pl.pallas_call(
+            finish,
+            out_shape=pltpu.VMEM((LATE, W, CB, LANES), jnp.bfloat16),
+            in_specs=[vmem, hbm],
+            out_specs=vmem,
+            scratch_shapes=[
+                pltpu.VMEM((LATE, PAIRS, TP, N_LOC, LANES), jnp.bfloat16),
+                dma((LATE, TP)), dma((LATE, TP)), dma((3, TP)), dma((3, TP)), pltpu.SemaphoreType.REGULAR((2,)),
+            ],
+            compiler_params=pltpu.CompilerParams(collective_id=1, has_side_effects=True, vmem_limit_bytes=12 * 2**20),
+        )(z, token)
+        out, _ = pl.pallas_call(
+            functools.partial(write, SPLIT, LATE, 2), out_shape=written, in_specs=[vmem, hbm], out_specs=(hbm, hbm), scratch_shapes=[dma((LATE // 2,))], input_output_aliases={1: 0}, compiler_params=small)(late, out)
         return jnp.transpose(out, (3, 0, 1, 2))
 
     return jax.shard_map(local_step, mesh=mesh, in_specs=(P(("pp", "tp")), P(None, None, "tp", None), P("tp"), P("tp")),

time: 291 us -> 288 us (0.990)
  the two profiles are of different devices: /device:TPU:1 before, /device:TPU:0 now
where the time goes in v5:
time: 288 us; the launch traced here: 287 us
  Pallas kernels  287 us (100%)
    pallas_call x1, Pallas kernels, local_step(): pl.pallas_call(kernel, out_shape=(pltpu.VMEM((SPLIT, W, CB, LANES), jnp.b...  218 us
    pallas_call x1, Pallas kernels, local_step(): pl.pallas_call(finish, out_shape=pltpu.VMEM((LATE, W, CB, LANES), jnp.bfl...  63.8 us

profile of v5, /device:TPU:0, one launch (start us, length us, event | category | flops | bytes accessed | tf_op | source)
XLA Modules:
  0.0 287.4 jit_solution(14697088713230459218)
XLA Ops:
  0.0 218.1 %shard_map.46 = (bf16[20,28,64,128]{3,2,1,0:T(8,128)(2,1)S(1)}, bf16[28,14,4,32,128]{4,3,2,1,0:T(8,128)(2,1)S(1)}) custom-call(bf16[28,28,32,256]{3,2,1,0:T(8,128)(2,1)} %bitcast.5, bf16[9,64,256]{2,1,0:T(8,128)(2,1)} %bitcast.6, f32[1,64]{1,0:T(1,128)} %bitcast.7, f32[1,64]{1,0:T(1,128)} %bitcast.8), custom_call_target="tpu_custom_call" | custom-call | tf_op jit(solution)/shard_map/pallas_call | solution.py:419
  218.1 3.6 %shard_map.47 = (bf16[28,28,64,128]{3,2,1,0:T(8,128)(2,1)}, f32[8,128]{1,0:T(8,128)S(1)}) custom-call(bf16[20,28,64,128]{3,2,1,0:T(8,128)(2,1)S(1)} %get-tuple-element.11.src), custom_call_target="tpu_custom_call" | custom-call | tf_op jit(solution)/shard_map/pallas_call | solution.py:437
  221.7 63.8 %shard_map.48.src = bf16[8,28,64,128]{3,2,1,0:T(8,128)(2,1)S(1)} custom-call(bf16[28,14,4,32,128]{4,3,2,1,0:T(8,128)(2,1)S(1)} %get-tuple-element.10.z, f32[8,128]{1,0:T(8,128)S(1)} %get-tuple-element.12._), custom_call_target="tpu_custom_call" | custom-call | tf_op jit(solution)/shard_map/pallas_call | solution.py:439
  285.6 1.9 shard_map.49

commit v6 on v5

--- a/solution.py
+++ b/solution.py
@@ -18,18 +18,19 @@
 G = 4
 GROUPS = H // G
 LAST = H - 1
-SPLIT = 20
-ODD_SPLIT = 24
+SOON, LATER = 1, 0
+SPLIT = 23
+LATER_SPLIT = 27
 LATE = H - SPLIT
 PARTS = ((0, 3, 3), (0, 6, 3), (0, 0, 3), (1, 0, 9))
 ORDER = (1, 0)
 FIRST = ((0, 0), (1, 0), (0, 1), (1, 1))
 REST = ((2, 0), (2, 1), (3, 0), (3, 1))
 HEAD = ((0, 7), (7, 7))
-ROWS = ((1, 1), (2, 2), (4, 4), (8, 8), (16, 4))
-ODD_ROWS = (SPLIT, ODD_SPLIT - SPLIT)
-LATE_EVEN = ((0, 4), (4, 2), (6, 1))
-LATE_ODD = ((4, 2), (6, 1))
+ROWS = ((1, 1), (2, 2), (4, 4), (8, 8), (16, 7))
+LATER_ROWS = (SPLIT, LATER_SPLIT - SPLIT)
+LATE_SOON = ((0, 4),)
+LATE_LATER = ()
 TAIL = ((0, 7), (7, 5), (12, 2))
 
 
@@ -224,27 +225,27 @@
                 def _():
                     send(first, rows, (0, 1))
 
-            last = jnp.logical_and(own, core == 1)
+            last = jnp.logical_and(own, core == LATER)
 
             @pl.when(h == SPLIT - 1)
             def _():
-                send(*ROWS[-1], (0,))
+                send(*ROWS[-1], (SOON,))
 
             @pl.when(jnp.logical_and(h == SPLIT - 1, jnp.logical_not(last)))
             def _():
-                send(*ROWS[-1], (1,))
-
-            @pl.when(jnp.logical_and(h == ODD_SPLIT - 1, core == 1))
-            def _():
-                send(*ODD_ROWS, (0,))
-
-            @pl.when(jnp.logical_and(h == ODD_SPLIT - 1, last))
-            def _():
-                send(*ROWS[-1], (1,))
-
-            @pl.when(jnp.logical_and(h == ODD_SPLIT - 1, core == 1))
-            def _():
-                send(*ODD_ROWS, (1,))
+                send(*ROWS[-1], (LATER,))
+
+            @pl.when(jnp.logical_and(h == LATER_SPLIT - 1, core == LATER))
+            def _():
+                send(*LATER_ROWS, (SOON,))
+
+            @pl.when(jnp.logical_and(h == LATER_SPLIT - 1, last))
+            def _():
+                send(*ROWS[-1], (LATER,))
+
+            @pl.when(jnp.logical_and(h == LATER_SPLIT - 1, core == LATER))
+            def _():
+                send(*LATER_ROWS, (LATER,))
             return 0
         lax.fori_loop(1, 2 * H, step, 0)
 
@@ -268,9 +269,9 @@
             for first, rows in ROWS:
                 z_copy(first, rows, t, tp).wait_send()
 
-            @pl.when(core == 1)
-            def _():
-                z_copy(*ODD_ROWS, t, tp).wait_send()
+            @pl.when(core == LATER)
+            def _():
+                z_copy(*LATER_ROWS, t, tp).wait_send()
 
     @pl.when(pp == 1)
     def _():
@@ -290,8 +291,8 @@
             for s in range(TP):
                 z_copy(first, rows, s, s).wait_recv()
             turn_rows(first, rows)
-        for s in (1, 3):
-            z_copy(*ODD_ROWS, s, s).wait_recv()
+        for s in (LATER, 2 + LATER):
+            z_copy(*LATER_ROWS, s, s).wait_recv()
 
 
 def turn(block, out, h, p):
@@ -304,7 +305,7 @@
     pp, tp = lax.axis_index("pp"), lax.axis_index("tp")
     core = tp % 2
     source = pp == 0
-    even = core == 0
+    soon = core == SOON
 
     def z_copy(first, rows, t, owner):
         return pltpu.make_async_remote_copy(
@@ -327,17 +328,17 @@
             for target in targets:
                 pl.semaphore_signal(barrier, inc=1, device_id=target, device_id_type=MESH)
 
-    greet(source & even, [(1, 0), (1, 2), (1, 1), (1, 3), (0, lax.rem(tp + 2, TP))])
-    greet(source & ~even, [(1, 1), (1, 3)])
-    greet(~source & even, [(0, 1), (0, 3)])
-    pl.semaphore_wait(barrier, jnp.where(source, jnp.where(even, 1, 2), jnp.where(even, 2, 4)))
-
-    @pl.when(~source & even)
-    def _():
-        for t in (0, 2):
+    greet(source & soon, [(1, 0), (1, 1), (1, 2), (1, 3), (0, lax.rem(tp + 2, TP))])
+    greet(source & ~soon, [(1, LATER), (1, 2 + LATER)])
+    greet(~source & soon, [(0, LATER), (0, 2 + LATER)])
+    pl.semaphore_wait(barrier, jnp.where(source, jnp.where(soon, 1, 2), jnp.where(soon, 2, 4)))
+
+    @pl.when(~source & soon)
+    def _():
+        for t in (SOON, 2 + SOON):
             pl.semaphore_signal(ready.at[0], inc=1, device_id=(0, t), device_id_type=MESH)
 
-    @pl.when(~source & ~even)
+    @pl.when(~source & ~soon)
     def _():
         for t in range(TP):
             pl.semaphore_signal(ready.at[1], inc=1, device_id=(0, t), device_id_type=MESH)
@@ -347,18 +348,18 @@
             for c in a:
                 c.start()
 
-    @pl.when(source & even)
+    @pl.when(source & soon)
     def _():
         pl.semaphore_wait(ready.at[0], 2)
-        sends(LATE_EVEN, 0)
+        sends(LATE_SOON, SOON)
         pl.semaphore_wait(ready.at[1], 2)
-        sends(LATE_EVEN, 1)
-
-    @pl.when(source & ~even)
-    def _():
-        sends(LATE_ODD, 0)
+        sends(LATE_SOON, LATER)
+
+    @pl.when(source & ~soon)
+    def _():
+        sends(LATE_LATER, SOON)
         pl.semaphore_wait(ready.at[1], 2)
-        sends(LATE_ODD, 1)
+        sends(LATE_LATER, LATER)
 
     @pl.when(source)
     def _():
@@ -366,7 +367,7 @@
             out[h] = jnp.zeros((W, CB, LANES), jnp.bfloat16)
             return 0
         lax.fori_loop(0, LATE, clear, 0)
-        for rows, where in ((LATE_EVEN, even), (LATE_ODD, ~even)):
+        for rows, where in ((LATE_SOON, soon), (LATE_LATER, ~soon)):
             @pl.when(where)
             def _():
                 for t in range(TP):
@@ -375,16 +376,16 @@
 
     @pl.when(~source)
     def _():
-        for s in (0, 2):
-            z_copy(*LATE_EVEN[0], s, s).wait_recv()
+        for s in (SOON, 2 + SOON):
+            z_copy(*LATE_SOON[0], s, s).wait_recv()
 
         def mixed(h, _):
             for p in range(PAIRS):
-                parts = [got[h, p, s] if s % 2 == 0 else z[SPLIT + h, p, s] for s in range(TP)]
+                parts = [got[h, p, s] if s % 2 == SOON else z[SPLIT + h, p, s] for s in range(TP)]
                 turn(jnp.concatenate(parts, axis=0), out, h, p)
             return 0
-        lax.fori_loop(0, ODD_SPLIT - SPLIT, mixed, 0)
-        for first, rows in LATE_ODD:
+        lax.fori_loop(0, LATER_SPLIT - SPLIT, mixed, 0)
+        for first, rows in LATE_LATER:
             for s in range(TP):
                 z_copy(first, rows, s, s).wait_recv()
 
@@ -430,12 +431,12 @@
                 dma((H,)), dma((2,)), dma((4, 3)), dma((4, TP)), dma((TP,)), dma((TP,)), dma((H, TP)), dma((H, TP)),
                 dma((2, TP)), dma((2, TP)), pltpu.VMEM((2, 1, CB), jnp.float32), dma((2,)), pltpu.SemaphoreType.REGULAR,
             ],
-            compiler_params=pltpu.CompilerParams(collective_id=0, has_side_effects=True, vmem_limit_bytes=44040192),
+            compiler_params=pltpu.CompilerParams(collective_id=0, has_side_effects=True, vmem_limit_bytes=42677043),
         )(x, w.reshape(9, C // TP, C), scale.reshape(1, CB), shift.reshape(1, CB))
         small = pltpu.CompilerParams(vmem_limit_bytes=2**20)
         written = (jax.ShapeDtypeStruct(shape, jnp.bfloat16), jax.ShapeDtypeStruct((8, LANES), jnp.float32))
         out, token = pl.pallas_call(
-            functools.partial(write, 0, SPLIT, 4), out_shape=written, in_specs=[vmem], out_specs=(hbm, hbm), scratch_shapes=[dma((SPLIT // 4,))], compiler_params=small)(early)
+            functools.partial(write, 0, SPLIT, 1), out_shape=written, in_specs=[vmem], out_specs=(hbm, hbm), scratch_shapes=[dma((SPLIT // 1,))], compiler_params=small)(early)
         late = pl.pallas_call(
             finish,
             out_shape=pltpu.VMEM((LATE, W, CB, LANES), jnp.bfloat16),
@@ -448,7 +449,7 @@
             compiler_params=pltpu.CompilerParams(collective_id=1, has_side_effects=True, vmem_limit_bytes=12 * 2**20),
         )(z, token)
         out, _ = pl.pallas_call(
-            functools.partial(write, SPLIT, LATE, 2), out_shape=written, in_specs=[vmem, hbm], out_specs=(hbm, hbm), scratch_shapes=[dma((LATE // 2,))], input_output_aliases={1: 0}, compiler_params=small)(late, out)
+            functools.partial(write, SPLIT, LATE, 1), out_shape=written, in_specs=[vmem, hbm], out_specs=(hbm, hbm), scratch_shapes=[dma((LATE // 1,))], input_output_aliases={1: 0}, compiler_params=small)(late, out)
         return jnp.transpose(out, (3, 0, 1, 2))
 
     return jax.shard_map(local_step, mesh=mesh, in_specs=(P(("pp", "tp")), P(None, None, "tp", None), P("tp"), P("tp")),

time: 288 us -> 285 us (0.990)
  the two profiles are of different devices: /device:TPU:0 before, /device:TPU:1 now
where the time goes in v6:
time: 285 us
  Pallas kernels  285 us (100%)
    pallas_call x1, Pallas kernels, local_step(): pl.pallas_call(kernel, out_shape=(pltpu.VMEM((SPLIT, W, CB, LANES), jnp.b...  246 us
    pallas_call x1, Pallas kernels, local_step(): pl.pallas_call(finish, out_shape=pltpu.VMEM((LATE, W, CB, LANES), jnp.bfl...  33.2 us

profile of v6, /device:TPU:1, one launch (start us, length us, event | category | flops | bytes accessed | tf_op | source)
XLA Modules:
  0.0 285.2 jit_solution(2837045647031437375)
XLA Ops:
  0.0 246.4 %shard_map.46 = (bf16[23,28,64,128]{3,2,1,0:T(8,128)(2,1)S(1)}, bf16[28,14,4,32,128]{4,3,2,1,0:T(8,128)(2,1)S(1)}) custom-call(bf16[28,28,32,256]{3,2,1,0:T(8,128)(2,1)} %bitcast.5, bf16[9,64,256]{2,1,0:T(8,128)(2,1)} %bitcast.6, f32[1,64]{1,0:T(1,128)} %bitcast.7, f32[1,64]{1,0:T(1,128)} %bitcast.8), custom_call_target="tpu_custom_call" | custom-call | tf_op jit(solution)/shard_map/pallas_call | solution.py:420
  246.5 4.1 %shard_map.47 = (bf16[28,28,64,128]{3,2,1,0:T(8,128)(2,1)}, f32[8,128]{1,0:T(8,128)S(1)}) custom-call(bf16[23,28,64,128]{3,2,1,0:T(8,128)(2,1)S(1)} %get-tuple-element.11.src), custom_call_target="tpu_custom_call" | custom-call | tf_op jit(solution)/shard_map/pallas_call | solution.py:438
  250.6 33.2 %shard_map.48.src = bf16[5,28,64,128]{3,2,1,0:T(8,128)(2,1)S(1)} custom-call(bf16[28,14,4,32,128]{4,3,2,1,0:T(8,128)(2,1)S(1)} %get-tuple-element.10.z, f32[8,128]{1,0:T(8,128)S(1)} %get-tuple-element.12._), custom_call_target="tpu_custom_call" | custom-call | tf_op jit(solution)/shard_map/pallas_call | solution.py:440
  283.8 1.4 shard_map.49

commit v7 on v6

--- a/solution.py
+++ b/solution.py
@@ -27,11 +27,11 @@
 FIRST = ((0, 0), (1, 0), (0, 1), (1, 1))
 REST = ((2, 0), (2, 1), (3, 0), (3, 1))
 HEAD = ((0, 7), (7, 7))
-ROWS = ((1, 1), (2, 2), (4, 4), (8, 8), (16, 7))
+ROWS = ((1, 1), (2, 6), (8, 15))
 LATER_ROWS = (SPLIT, LATER_SPLIT - SPLIT)
 LATE_SOON = ((0, 4),)
 LATE_LATER = ()
-TAIL = ((0, 7), (7, 5), (12, 2))
+TAIL = ((0, 12), (12, 2))
 
 
 def kernel(act, w, scale, shift, out, buf, xpad, wf, sb, xsem, wlsem, wssem, wrsem, bssem, brsem, ssem, rsem, esem, fsem, vecs, vsem, ready):
@@ -444,7 +444,7 @@
             out_specs=vmem,
             scratch_shapes=[
                 pltpu.VMEM((LATE, PAIRS, TP, N_LOC, LANES), jnp.bfloat16),
-                dma((LATE, TP)), dma((LATE, TP)), dma((3, TP)), dma((3, TP)), pltpu.SemaphoreType.REGULAR((2,)),
+                dma((LATE, TP)), dma((LATE, TP)), dma((2, TP)), dma((2, TP)), pltpu.SemaphoreType.REGULAR((2,)),
             ],
             compiler_params=pltpu.CompilerParams(collective_id=1, has_side_effects=True, vmem_limit_bytes=12 * 2**20),
         )(z, token)

time: 285 us -> 285 us (level)
  no operation moved by 1% of the time
where the time goes in v7:
time: 285 us
  Pallas kernels  285 us (100%)
    pallas_call x1, Pallas kernels, local_step(): pl.pallas_call(kernel, out_shape=(pltpu.VMEM((SPLIT, W, CB, LANES), jnp.b...  246 us
    pallas_call x1, Pallas kernels, local_step(): pl.pallas_call(finish, out_shape=pltpu.VMEM((LATE, W, CB, LANES), jnp.bfl...  33.1 us

profile of v7, /device:TPU:1, one launch (start us, length us, event | category | flops | bytes accessed | tf_op | source)
XLA Modules:
  0.0 284.8 jit_solution(12686695616659022718)
XLA Ops:
  0.0 246.1 %shard_map.46 = (bf16[23,28,64,128]{3,2,1,0:T(8,128)(2,1)S(1)}, bf16[28,14,4,32,128]{4,3,2,1,0:T(8,128)(2,1)S(1)}) custom-call(bf16[28,28,32,256]{3,2,1,0:T(8,128)(2,1)} %bitcast.5, bf16[9,64,256]{2,1,0:T(8,128)(2,1)} %bitcast.6, f32[1,64]{1,0:T(1,128)} %bitcast.7, f32[1,64]{1,0:T(1,128)} %bitcast.8), custom_call_target="tpu_custom_call" | custom-call | tf_op jit(solution)/shard_map/pallas_call | solution.py:420
  246.1 4.1 %shard_map.47 = (bf16[28,28,64,128]{3,2,1,0:T(8,128)(2,1)}, f32[8,128]{1,0:T(8,128)S(1)}) custom-call(bf16[23,28,64,128]{3,2,1,0:T(8,128)(2,1)S(1)} %get-tuple-element.11.src), custom_call_target="tpu_custom_call" | custom-call | tf_op jit(solution)/shard_map/pallas_call | solution.py:438
  250.3 33.1 %shard_map.48.src = bf16[5,28,64,128]{3,2,1,0:T(8,128)(2,1)S(1)} custom-call(bf16[28,14,4,32,128]{4,3,2,1,0:T(8,128)(2,1)S(1)} %get-tuple-element.10.z, f32[8,128]{1,0:T(8,128)S(1)} %get-tuple-element.12._), custom_call_target="tpu_custom_call" | custom-call | tf_op jit(solution)/shard_map/pallas_call | solution.py:440
  283.4 1.4 shard_map.49

commit v8 on v7

--- a/solution.py
+++ b/solution.py
@@ -26,10 +26,10 @@
 ORDER = (1, 0)
 FIRST = ((0, 0), (1, 0), (0, 1), (1, 1))
 REST = ((2, 0), (2, 1), (3, 0), (3, 1))
-HEAD = ((0, 7), (7, 7))
+HEAD = ((0, 2), (2, 12))
 ROWS = ((1, 1), (2, 6), (8, 15))
 LATER_ROWS = (SPLIT, LATER_SPLIT - SPLIT)
-LATE_SOON = ((0, 4),)
+LATE_SOON = ((0, 2), (2, 2))
 LATE_LATER = ()
 TAIL = ((0, 12), (12, 2))
 
@@ -348,10 +348,16 @@
             for c in a:
                 c.start()
 
+    chip, far = tp // 2, 1 - tp // 2
+
     @pl.when(source & soon)
     def _():
         pl.semaphore_wait(ready.at[0], 2)
-        sends(LATE_SOON, SOON)
+        for c in copies(LATE_SOON, 2 * chip + SOON, tp):
+            c.start()
+        z_copy(*LATE_SOON[0], 2 * chip + SOON, tp).wait_send()
+        for c in copies(LATE_SOON, 2 * far + SOON, tp):
+            c.start()
         pl.semaphore_wait(ready.at[1], 2)
         sends(LATE_SOON, LATER)
 
@@ -370,14 +376,17 @@
         for rows, where in ((LATE_SOON, soon), (LATE_LATER, ~soon)):
             @pl.when(where)
             def _():
-                for t in range(TP):
+                for c in copies(rows[1:] if where is soon else rows, 2 * chip + SOON, tp):
+                    c.wait_send()
+                for t in (2 * chip + LATER, 2 * far, 2 * far + 1):
                     for c in copies(rows, t, tp):
                         c.wait_send()
 
     @pl.when(~source)
     def _():
         for s in (SOON, 2 + SOON):
-            z_copy(*LATE_SOON[0], s, s).wait_recv()
+            for piece in LATE_SOON:
+                z_copy(*piece, s, s).wait_recv()
 
         def mixed(h, _):
             for p in range(PAIRS):

time: 285 us -> 285 us (level)
  no operation moved by 1% of the time
where the time goes in v8:
time: 285 us; the launch traced here: 284 us
  Pallas kernels  284 us (100%)
    pallas_call x1, Pallas kernels, local_step(): pl.pallas_call(kernel, out_shape=(pltpu.VMEM((SPLIT, W, CB, LANES), jnp.b...  246 us
    pallas_call x1, Pallas kernels, local_step(): pl.pallas_call(finish, out_shape=pltpu.VMEM((LATE, W, CB, LANES), jnp.bfl...  33 us

profile of v8, /device:TPU:1, one launch (start us, length us, event | category | flops | bytes accessed | tf_op | source)
XLA Modules:
  0.0 284.5 jit_solution(1398765597165982441)
XLA Ops:
  0.0 245.9 %shard_map.46 = (bf16[23,28,64,128]{3,2,1,0:T(8,128)(2,1)S(1)}, bf16[28,14,4,32,128]{4,3,2,1,0:T(8,128)(2,1)S(1)}) custom-call(bf16[28,28,32,256]{3,2,1,0:T(8,128)(2,1)} %bitcast.5, bf16[9,64,256]{2,1,0:T(8,128)(2,1)} %bitcast.6, f32[1,64]{1,0:T(1,128)} %bitcast.7, f32[1,64]{1,0:T(1,128)} %bitcast.8), custom_call_target="tpu_custom_call" | custom-call | tf_op jit(solution)/shard_map/pallas_call | solution.py:429
  245.9 4.1 %shard_map.47 = (bf16[28,28,64,128]{3,2,1,0:T(8,128)(2,1)}, f32[8,128]{1,0:T(8,128)S(1)}) custom-call(bf16[23,28,64,128]{3,2,1,0:T(8,128)(2,1)S(1)} %get-tuple-element.11.src), custom_call_target="tpu_custom_call" | custom-call | tf_op jit(solution)/shard_map/pallas_call | solution.py:447
  250.0 33.0 %shard_map.48.src = bf16[5,28,64,128]{3,2,1,0:T(8,128)(2,1)S(1)} custom-call(bf16[28,14,4,32,128]{4,3,2,1,0:T(8,128)(2,1)S(1)} %get-tuple-element.10.z, f32[8,128]{1,0:T(8,128)S(1)} %get-tuple-element.12._), custom_call_target="tpu_custom_call" | custom-call | tf_op jit(solution)/shard_map/pallas_call | solution.py:449
  283.1 1.4 shard_map.49

commit v9 on v8

--- a/solution.py
+++ b/solution.py
@@ -458,7 +458,7 @@
             compiler_params=pltpu.CompilerParams(collective_id=1, has_side_effects=True, vmem_limit_bytes=12 * 2**20),
         )(z, token)
         out, _ = pl.pallas_call(
-            functools.partial(write, SPLIT, LATE, 1), out_shape=written, in_specs=[vmem, hbm], out_specs=(hbm, hbm), scratch_shapes=[dma((LATE // 1,))], input_output_aliases={1: 0}, compiler_params=small)(late, out)
+            functools.partial(write, SPLIT, LATE, 5), out_shape=written, in_specs=[vmem, hbm], out_specs=(hbm, hbm), scratch_shapes=[dma((LATE // 5,))], input_output_aliases={1: 0}, compiler_params=small)(late, out)
         return jnp.transpose(out, (3, 0, 1, 2))
 
     return jax.shard_map(local_step, mesh=mesh, in_specs=(P(("pp", "tp")), P(None, None, "tp", None), P("tp"), P("tp")),

time: 285 us -> 285 us (level)
  no operation moved by 1% of the time
where the time goes in v9:
time: 285 us; the launch traced here: 284 us
  Pallas kernels  284 us (100%)
    pallas_call x1, Pallas kernels, local_step(): pl.pallas_call(kernel, out_shape=(pltpu.VMEM((SPLIT, W, CB, LANES), jnp.b...  246 us
    pallas_call x1, Pallas kernels, local_step(): pl.pallas_call(finish, out_shape=pltpu.VMEM((LATE, W, CB, LANES), jnp.bfl...  33 us

profile of v9, /device:TPU:1, one launch (start us, length us, event | category | flops | bytes accessed | tf_op | source)
XLA Modules:
  0.0 284.5 jit_solution(7723026296450737160)
XLA Ops:
  0.0 245.9 %shard_map.46 = (bf16[23,28,64,128]{3,2,1,0:T(8,128)(2,1)S(1)}, bf16[28,14,4,32,128]{4,3,2,1,0:T(8,128)(2,1)S(1)}) custom-call(bf16[28,28,32,256]{3,2,1,0:T(8,128)(2,1)} %bitcast.5, bf16[9,64,256]{2,1,0:T(8,128)(2,1)} %bitcast.6, f32[1,64]{1,0:T(1,128)} %bitcast.7, f32[1,64]{1,0:T(1,128)} %bitcast.8), custom_call_target="tpu_custom_call" | custom-call | tf_op jit(solution)/shard_map/pallas_call | solution.py:429
  245.9 4.1 %shard_map.47 = (bf16[28,28,64,128]{3,2,1,0:T(8,128)(2,1)}, f32[8,128]{1,0:T(8,128)S(1)}) custom-call(bf16[23,28,64,128]{3,2,1,0:T(8,128)(2,1)S(1)} %get-tuple-element.11.src), custom_call_target="tpu_custom_call" | custom-call | tf_op jit(solution)/shard_map/pallas_call | solution.py:447
  250.0 33.0 %shard_map.48.src = bf16[5,28,64,128]{3,2,1,0:T(8,128)(2,1)S(1)} custom-call(bf16[28,14,4,32,128]{4,3,2,1,0:T(8,128)(2,1)S(1)} %get-tuple-element.10.z, f32[8,128]{1,0:T(8,128)S(1)} %get-tuple-element.12._), custom_call_target="tpu_custom_call" | custom-call | tf_op jit(solution)/shard_map/pallas_call | solution.py:449
  283.1 1.4 shard_map.49

commit v10 on v9

--- a/solution.py
+++ b/solution.py
@@ -26,7 +26,7 @@
 ORDER = (1, 0)
 FIRST = ((0, 0), (1, 0), (0, 1), (1, 1))
 REST = ((2, 0), (2, 1), (3, 0), (3, 1))
-HEAD = ((0, 2), (2, 12))
+HEAD = ((0, 3), (3, 11))
 ROWS = ((1, 1), (2, 6), (8, 15))
 LATER_ROWS = (SPLIT, LATER_SPLIT - SPLIT)
 LATE_SOON = ((0, 2), (2, 2))

time: 285 us -> 285 us (level)
  no operation moved by 1% of the time
where the time goes in v10:
time: 285 us
  Pallas kernels  285 us (100%)
    pallas_call x1, Pallas kernels, local_step(): pl.pallas_call(kernel, out_shape=(pltpu.VMEM((SPLIT, W, CB, LANES), jnp.b...  246 us
    pallas_call x1, Pallas kernels, local_step(): pl.pallas_call(finish, out_shape=pltpu.VMEM((LATE, W, CB, LANES), jnp.bfl...  33.1 us

profile of v10, /device:TPU:1, one launch (start us, length us, event | category | flops | bytes accessed | tf_op | source)
XLA Modules:
  0.0 284.6 jit_solution(11606582691007554670)
XLA Ops:
  0.0 245.9 %shard_map.46 = (bf16[23,28,64,128]{3,2,1,0:T(8,128)(2,1)S(1)}, bf16[28,14,4,32,128]{4,3,2,1,0:T(8,128)(2,1)S(1)}) custom-call(bf16[28,28,32,256]{3,2,1,0:T(8,128)(2,1)} %bitcast.5, bf16[9,64,256]{2,1,0:T(8,128)(2,1)} %bitcast.6, f32[1,64]{1,0:T(1,128)} %bitcast.7, f32[1,64]{1,0:T(1,128)} %bitcast.8), custom_call_target="tpu_custom_call" | custom-call | tf_op jit(solution)/shard_map/pallas_call | solution.py:429
  245.9 4.1 %shard_map.47 = (bf16[28,28,64,128]{3,2,1,0:T(8,128)(2,1)}, f32[8,128]{1,0:T(8,128)S(1)}) custom-call(bf16[23,28,64,128]{3,2,1,0:T(8,128)(2,1)S(1)} %get-tuple-element.11.src), custom_call_target="tpu_custom_call" | custom-call | tf_op jit(solution)/shard_map/pallas_call | solution.py:447
  250.0 33.1 %shard_map.48.src = bf16[5,28,64,128]{3,2,1,0:T(8,128)(2,1)S(1)} custom-call(bf16[28,14,4,32,128]{4,3,2,1,0:T(8,128)(2,1)S(1)} %get-tuple-element.10.z, f32[8,128]{1,0:T(8,128)S(1)} %get-tuple-element.12._), custom_call_target="tpu_custom_call" | custom-call | tf_op jit(solution)/shard_map/pallas_call | solution.py:449
  283.2 1.4 shard_map.49
